TPU v7x, 128 devices: a whole 4x4x4 slice. The times are simulated.
128 devices in a mesh: seq: 32 (over y, z, core), head: 4 (over x).
Axes of the slice: x: 4, y: 4, z: 4, core: 2. Of those that a mesh axis runs over, the one named last changes fastest.
Arguments:
- inputs: bfloat16 [8192, 2048], P('seq', 'head'), may hold values from -6 to 6
- w_query: bfloat16 [2048, 2048], P(None, 'head'), may hold values from -0.125 to 0.125
- w_key: bfloat16 [2048, 2048], P(None, 'head'), may hold values from -0.125 to 0.125
- w_value: bfloat16 [2048, 2048], P(None, 'head'), may hold values from -0.125 to 0.125
- sketch: float32 [2, 64, 32], replicated, may hold values from -0.75 to 0.75
- prefix_state: float32 [32, 1024, 64], P('head'), may hold values from -112 to 112
- prefix_norm: float32 [32, 1024], P('head'), as said below
- d_attn: bfloat16 [8192, 2048], P('seq', 'head'), may hold values from -256 to 256
- d_state_end: float32 [32, 1024, 64], P('head'), may hold values from -6 to 6
- d_norm_end: float32 [32, 1024], P('head'), may hold values from -4 to 4
Outputs:
- d_input: bfloat16 [8192, 2048], P('seq', 'head')
- d_query: bfloat16 [8192, 2048], P('seq', 'head')
- d_key: bfloat16 [8192, 2048], P('seq', 'head')
- d_value: bfloat16 [8192, 2048], P('seq', 'head')
- d_prefix_state: float32 [32, 1024, 64], P('head')
- d_prefix_norm: float32 [32, 1024], P('head')
Inputs may be any that keep to these rules, and one draw needn't show every extreme that they name: For every head, prefix_norm laid out as a 32 x 32 matrix is symmetric positive semidefinite.
All inputs are finite; a program needn't handle non-finite values.
Results may differ from a plain program's by a relative error of at most 0.012.
Values may be sent and summed in bfloat16 or wider, within the bound.
A program may use at most 192 MiB of HBM per device.

v0:
```python
from functools import partial

import jax
import jax.numpy as jnp
from jax import lax
from jax.sharding import Mesh
from jax.sharding import PartitionSpec as P

SEQ = ("seq_0", "seq_1", "seq_2")


HIGHEST_PRECISION = lax.Precision.HIGHEST


def laid_out(parts, dim):
    lengths = list(parts.shape[1:])
    lengths[dim] *= parts.shape[0]
    return jnp.moveaxis(parts, 0, dim).reshape(lengths)


def copy_for_each(value, axis):
    count = lax.axis_size(axis)
    return lax.all_to_all(
        jnp.broadcast_to(value[None], (count, *value.shape)), axis, 0, 0, tiled=True
    )


def gathered_copies(value, axis, dim):
    return laid_out(copy_for_each(value, axis), dim)


def neutral_like(value, identity):
    return jax.tree.map(
        lambda a, e: jnp.broadcast_to(jnp.asarray(e, a.dtype), a.shape), value, identity
    )


def prefix_by_axis(value, axes, combine, identity):
    before = start = neutral_like(value, identity)
    subtotal = value
    for axis in reversed(axes):
        count, index = (lax.axis_size(axis), lax.axis_index(axis))
        pieces = jax.tree.map(
            lambda part, kind: lax.all_gather(part.astype(kind), axis),
            subtotal,
            (jnp.bfloat16, jnp.bfloat16),
        )
        inside, subtotal = (start, start)
        for k in range(count):
            passed = k < index
            subtotal = combine(
                subtotal, jax.tree.map(lambda part, own: part[k].astype(own.dtype), pieces, value)
            )
            inside = jax.tree.map(lambda new, old: jnp.where(passed, new, old), subtotal, inside)
        before = combine(inside, before)
    return before


def carried_in(value, axes, combine, identity):
    before = start = neutral_like(value, identity)
    subtotal = value
    for axis in reversed(axes):
        count, index = (lax.axis_size(axis), lax.axis_index(axis))
        pieces = jax.tree.map(
            lambda part, kind: lax.all_gather(part.astype(kind), axis),
            subtotal,
            jax.tree.map(lambda a: jnp.bfloat16 if a.dtype == jnp.float32 else a.dtype, value),
        )
        inside, subtotal = (start, start)
        for k in reversed(range(count)):
            passed = k > index
            subtotal = combine(
                subtotal, jax.tree.map(lambda part, own: part[k].astype(own.dtype), pieces, value)
            )
            inside = jax.tree.map(lambda new, old: jnp.where(passed, new, old), subtotal, inside)
        before = combine(inside, before)
    return before


def in_blocks(value, dim, count):
    before, after = (value.shape[:dim], value.shape[dim + 1 :])
    return jnp.moveaxis(value.reshape(*before, count, -1, *after), dim, 0)


def sum_at_owner(value, axis, dim):
    count = lax.axis_size(axis)
    parts = lax.all_to_all(in_blocks(value, dim, count), axis, 0, 0, tiled=True)
    return jnp.sum(parts.astype(jnp.float32), axis=0)


def packed_total(arrays, axis):
    ends = [0]
    for a in arrays:
        ends.append(ends[-1] + a.size)
    subtotal = lax.psum(jnp.concatenate([a.ravel() for a in arrays]), axis)
    return tuple((subtotal[b:e].reshape(a.shape) for a, b, e in zip(arrays, ends, ends[1:])))


def sketch_map(values, sketch):
    left_map = jnp.einsum("hbd,de->hbe", values, sketch[0], precision=HIGHEST_PRECISION)
    right_map = jnp.einsum("hbd,de->hbe", values, sketch[1], precision=HIGHEST_PRECISION)
    return left_map * right_map * sketch.shape[2] ** (-0.5)


def square_features(sketched):
    outer_prod = sketched[:, :, :, None] * sketched[:, :, None, :]
    return outer_prod.reshape(sketched.shape[0], sketched.shape[1], -1)


def attend_block(carried, block_data, sketch):
    value_state, norm_state = carried
    query_block, key_block, value_block = block_data
    sketch_query = sketch_map(query_block, sketch)
    sketch_key = sketch_map(key_block, sketch)
    feat_query = square_features(sketch_query)
    block_size = query_block.shape[1]
    causal = lax.broadcasted_iota(jnp.int32, (block_size, block_size), 0) >= lax.broadcasted_iota(
        jnp.int32, (block_size, block_size), 1
    )
    dot_prod = jnp.einsum("hid,hjd->hij", sketch_query, sketch_key, precision=HIGHEST_PRECISION)
    scores = jnp.where(causal, dot_prod * dot_prod, jnp.zeros_like(dot_prod))
    numerator = jnp.einsum("hif,hfd->hid", feat_query, value_state, precision=HIGHEST_PRECISION)
    numerator = numerator + jnp.einsum(
        "hij,hjd->hid", scores, value_block, precision=HIGHEST_PRECISION
    )
    denominator = (
        1.0
        + jnp.einsum("hif,hf->hi", feat_query, norm_state, precision=HIGHEST_PRECISION)
        + scores.sum(-1)
    )
    outputs = numerator / denominator[:, :, None]
    feat_key = square_features(sketch_key)
    value_state = value_state + jnp.einsum(
        "hjf,hjd->hfd", feat_key, value_block, precision=HIGHEST_PRECISION
    )
    norm_state = norm_state + feat_key.sum(1)
    return ((value_state, norm_state), outputs)


def split_blocks(values, block_size):
    head_count, total_rows, depth_size = values.shape
    return values.reshape(head_count, total_rows // block_size, block_size, depth_size).transpose(
        1, 0, 2, 3
    )


def join_blocks(values):
    block_count, head_count, block_size, depth_size = values.shape
    return values.transpose(1, 0, 2, 3).reshape(head_count, block_count * block_size, depth_size)


def attend_local(query, key, value, value_state, norm_state, sketch):
    block_size = min(query.shape[1], 512)
    block_step = partial(attend_block, sketch=sketch)
    carried, outputs = lax.scan(
        block_step,
        (value_state, norm_state),
        (
            split_blocks(query, block_size),
            split_blocks(key, block_size),
            split_blocks(value, block_size),
        ),
    )
    return join_blocks(outputs)


def local_totals(key, value, sketch):
    block_size = min(key.shape[1], 512)

    def add_block(carried, block_data):
        key_block, value_block = block_data
        feat_key = square_features(sketch_map(key_block, sketch))
        state_sum = carried[0] + jnp.einsum(
            "hjf,hjd->hfd", feat_key, value_block, precision=HIGHEST_PRECISION
        )
        return ((state_sum, carried[1] + feat_key.sum(1)), None)

    feat_size = sketch.shape[2] * sketch.shape[2]
    start_state = jnp.zeros((key.shape[0], feat_size, key.shape[2]), jnp.float32)
    start_norm = jnp.zeros((key.shape[0], feat_size), jnp.float32)
    carried, unused = lax.scan(
        add_block,
        (start_state, start_norm),
        (split_blocks(key, block_size), split_blocks(value, block_size)),
    )
    return carried


def add_pair(earlier, later):
    return (earlier[0] + later[0], earlier[1] + later[1])


def pull_weight(gradient, weight):
    return lax.dot_general(
        gradient, weight, (((1,), (1,)), ((), ())), preferred_element_type=jnp.float32
    )


def body(
    inputs,
    w_query,
    w_key,
    w_value,
    sketch,
    prefix_state,
    prefix_norm,
    d_attn,
    d_state_end,
    d_norm_end,
):
    tok_rows = inputs.shape[0]
    width = w_query.shape[1]
    head_count = prefix_state.shape[0]
    head_size = width // head_count
    shard_cols = gathered_copies(inputs, "head", 1)
    query, key, value = tuple(
        (
            jnp.dot(shard_cols, weight, preferred_element_type=jnp.float32)
            for weight in (w_query, w_key, w_value)
        )
    )

    def to_heads(values):
        return (
            values.reshape(tok_rows, head_count, head_size).transpose(1, 0, 2).astype(jnp.float32)
        )

    def flatten(values):
        return values.transpose(1, 0, 2).reshape(tok_rows, width).astype(jnp.bfloat16)

    query_heads = to_heads(lax.optimization_barrier(query.astype(jnp.bfloat16)))
    key_heads = to_heads(lax.optimization_barrier(key.astype(jnp.bfloat16)))
    value_heads = to_heads(lax.optimization_barrier(value.astype(jnp.bfloat16)))

    def totals_of(key_in, value_in):
        return local_totals(key_in, value_in, sketch)

    (state_here, norm_here), pull_totals = jax.vjp(totals_of, key_heads, value_heads)
    zero_state = jnp.zeros_like(prefix_state)
    zero_norm = jnp.zeros_like(prefix_norm)
    state_before, norm_before = prefix_by_axis(
        (state_here, norm_here), SEQ, add_pair, (zero_state, zero_norm)
    )
    state_prev = prefix_state + state_before
    norm_prev = prefix_norm + norm_before

    def outputs_of(query_in, key_in, value_in, state_in, norm_in):
        return attend_local(query_in, key_in, value_in, state_in, norm_in, sketch)

    unused, pull_local = jax.vjp(
        outputs_of, query_heads, key_heads, value_heads, state_prev, norm_prev
    )
    grad_query, grad_key, grad_value, cot_state, cot_norm = pull_local(to_heads(d_attn))
    d_query = flatten(grad_query)
    state_after, norm_after = carried_in(
        (cot_state, cot_norm), SEQ, add_pair, (zero_state, zero_norm)
    )
    state_after = d_state_end + state_after
    norm_after = d_norm_end + norm_after
    extra_key, extra_value = pull_totals((state_after, norm_after))
    d_key = flatten(grad_key + extra_key)
    d_value = flatten(grad_value + extra_value)
    whole_term = (
        pull_weight(d_query, w_query) + pull_weight(d_key, w_key) + pull_weight(d_value, w_value)
    )
    d_input = sum_at_owner(whole_term.astype(jnp.bfloat16), "head", 1).astype(jnp.bfloat16)
    total_state, total_norm = tuple(
        (
            part.astype(jnp.float32)
            for part in packed_total(
                (cot_state.astype(jnp.bfloat16), cot_norm.astype(jnp.bfloat16)), SEQ
            )
        )
    )
    d_prefix_state = d_state_end + total_state
    d_prefix_norm = d_norm_end + total_norm
    return (d_input, d_query, d_key, d_value, d_prefix_state, d_prefix_norm)


def solution(mesh):
    finer = Mesh(
        mesh.devices.reshape(4, 4, 2, mesh.shape["head"]), ("seq_0", "seq_1", "seq_2", "head")
    )
    return jax.shard_map(
        body,
        mesh=finer,
        in_specs=(
            P(SEQ, "head"),
            P(None, "head"),
            P(None, "head"),
            P(None, "head"),
            P(),
            P("head", None, None),
            P("head", None),
            P(SEQ, "head"),
            P("head", None, None),
            P("head", None),
        ),
        out_specs=(
            P(SEQ, "head"),
            P(SEQ, "head"),
            P(SEQ, "head"),
            P(SEQ, "head"),
            P("head", None, None),
            P("head", None),
        ),
        check_vma=False,
    )
```

profile of v0, /device:TPU:1, one launch (start us, length us, event | category | flops | bytes accessed | tf_op | source)
XLA Modules:
  0.0 523.1 jit_solution(4007921592596742459)
XLA Ops:
  7.2 1.2 copy.56
  8.4 1.0 broadcast_in_dim.136
  9.5 4.8 all-to-all-start
  14.5 14.2 %all-to-all-done = bf16[4,256,512]{1,2,0:T(8,128)(2,1)} async-done(((bf16[4,256,512]{1,2,0:T(8,128)(2,1)}), bf16[4,256,512]{1,2,0:T(8,128)(2,1)}, u32[]{:S(2)}, u32[]{:S(2)}) %all-to-all-start) | async-done | bytes 1048608 | tf_op jit(solution)/shard_map/all_to_all | solution.py:23
  28.7 2.6 convolution_convert_fusion.2
  31.4 3.4 convolution_convert_fusion.3
  34.8 2.0 convolution_convert_fusion.4
  36.9 1.1 copy.58
  39.0 1.0 multiply_multiply_fusion.1
  39.9 1.9 multiply_multiply_fusion
  41.9 3.4 fusion.49
  45.3 5.6 %multiply_reduce_fusion.2 = (f32[8,256,32]{1,2,0:T(8,128)}, bf16[8,32,32]{2,1,0:T(8,128)(2,1)}, f32[8,256,32]{1,2,0:T(8,128)}, f32[8,256,32,32]{1,3,2,0:T(8,128)}) fusion(f32[8,256,32]{1,2,0:T(8,128)S(1)} %get-tuple-element.403, f32[8,256,1024]{1,2,0:T(8,128)S(1)} %fusion.49, f32[8,256,32,32]{1,3,2,0:T(8,128)S(1)} %bitcast.171), kind=kLoop, calls=%fused_computation.2 | loop fusion | flops 12443648 | bytes 25968640 | tf_op jit(solution)/shard_map/transpose(jvp())/while/body/eval_jaxpr/reduce_sum | solution.py:106
  51.9 3.3 all_gather.54
  55.8 10.4 %all_gather.55 = bf16[4,8,1024]{2,1,0:T(8,128)(2,1)S(1)} all-gather(bf16[1,8,1024]{2,1,0:T(8,128)(2,1)S(1)} %fusion.92), channel_id=1, replica_groups=mesh['seq_0'=4,'seq_1'=4,'seq_2'=2,'head'=4] {'seq_1'}, dimensions={0}, use_global_device_ids=true | all-gather | bytes 81920 | tf_op jit(solution)/shard_map/all_gather | solution.py:44
  66.8 10.5 %all_gather.56 = bf16[4,8,1024]{2,1,0:T(8,128)(2,1)} all-gather(bf16[1,8,1024]{2,1,0:T(8,128)(2,1)S(1)} %fusion.91), channel_id=1, replica_groups=mesh['seq_0'=4,'seq_1'=4,'seq_2'=2,'head'=4] {'seq_0'}, dimensions={0}, use_global_device_ids=true | all-gather | bytes 81920 | tf_op jit(solution)/shard_map/all_gather | solution.py:44
  77.3 8.7 %convolution_convert_fusion.1 = bf16[8,1024,64]{1,2,0:T(8,128)(2,1)} fusion(f32[8,256,1024]{1,2,0:T(8,128)} %bitcast.168, bf16[8,256,64]{1,2,0:T(8,128)(2,1)S(1)} %bitcast.176), kind=kOutput, calls=%fused_computation.64 | convolution fusion | flops 1611137024 | bytes 9699328 | tf_op jit(solution)/shard_map/jvp()/while/body/eval_jaxpr/hjf,hjd->hfd/dot_general | solution.py:173
  87.1 3.3 fusion.32
  90.4 1.1 broadcast_multiply_fusion.1
  91.5 4.4 fusion.87
  95.9 18.2 %convolution_convert_fusion = bf16[8,1024,64]{1,2,0:T(8,128)(2,1)} fusion(f32[8,256,1024]{1,2,0:T(8,128)S(1)} %bitcast.165, f32[8,256]{1,0:T(8,128)S(1)} %get-tuple-element.397, f32[256,512]{0,1:T(8,128)S(1)} %copy.59), kind=kOutput, calls=%fused_computation.63 | convolution fusion | flops 1611268096 | bytes 9969664 | tf_op jit(solution)/shard_map/transpose(jvp())/while/body/eval_jaxpr/hif,hfd->hid/dot_general | solution.py:122
  114.2 3.0 fusion.45
  117.3 14.7 %all-gather.20.cloned.1.call-done = bf16[16,1024,64]{1,2,0:T(8,128)(2,1)} async-done(((bf16[8,1024,64]{1,2,0:T(8,128)(2,1)}), bf16[16,1024,64]{1,2,0:T(8,128)(2,1)}) %all-gather.20.cloned.1.call-update) | async-done | bytes 2097168 | tf_op jit(solution)/shard_map/all_gather | solution.py:65
  132.0 2.9 fusion.46
  135.0 47.9 %all-gather.10.cloned.1.call-done = bf16[4,8,1024,64]{2,3,1,0:T(8,128)(2,1)} async-done(((bf16[1,8,1024,64]{2,3,1,0:T(8,128)(2,1)}), bf16[4,8,1024,64]{2,3,1,0:T(8,128)(2,1)}) %all-gather.10.cloned.1.call-update) | async-done | bytes 4194320 | tf_op jit(solution)/shard_map/all_gather | solution.py:44
  182.9 4.1 fusion.29
  187.1 46.0 %all-gather.14.cloned.1.call-done = bf16[4,8,1024,64]{2,3,1,0:T(8,128)(2,1)} async-done(((bf16[1,8,1024,64]{2,3,1,0:T(8,128)(2,1)}), bf16[4,8,1024,64]{2,3,1,0:T(8,128)(2,1)}) %all-gather.14.cloned.1.call-update) | async-done | bytes 4194320 | tf_op jit(solution)/shard_map/all_gather | solution.py:65
  233.0 4.1 fusion.28
  237.2 3.8 copy.76
  241.0 2.8 copy.75
  243.8 4.0 reshape.397
  247.8 8.6 %fusion.47 = f32[8,256,64]{1,2,0:T(8,128)} fusion(f32[8,256,1024]{1,2,0:T(8,128)} %bitcast.169), kind=kOutput, calls=%fused_computation.90 | convolution fusion | flops 1610612736 | bytes 8912896 | tf_op jit(solution)/shard_map/transpose(jvp())/while/body/eval_jaxpr/hjf,hjd->hfd/dot_general | solution.py:133
  256.4 26.6 %all-gather.12.cloned.1.call-done = bf16[4,8,1024,64]{2,3,1,0:T(8,128)(2,1)} async-done(((bf16[1,8,1024,64]{2,3,1,0:T(8,128)(2,1)}), bf16[4,8,1024,64]{2,3,1,0:T(8,128)(2,1)}) %all-gather.12.cloned.1.call-update) | async-done | bytes 4194320 | tf_op jit(solution)/shard_map/all_gather | solution.py:44
  283.0 5.9 %fusion.8 = f32[8,1024,64]{1,2,0:T(8,128)S(1)} fusion(f32[8,1024,64]{1,2,0:T(8,128)} %param.15, bf16[4,8,1024,64]{2,3,1,0:T(8,128)(2,1)} %all-gather.12.cloned.1.call-done, pred[]{:T(512)S(6)} %gt.38, pred[]{:T(512)S(6)} %gt.39, pred[]{:T(512)S(6)} %gt.34, pred[]{:T(512)S(6)} %gt.30, pred[]{:T(512)S(6)} %gt.37, pred[]{:T(512)S(6)} %gt.36, pred[]{:T(512)S(6)} %gt.35, ...), kind=kLoop, calls=%fused_computation.32 | loop fusion | flops 15728640 | bytes 14680074 | tf_op jit(solution)/shard_map/add | solution.py:244
  288.9 8.5 %fusion.128 = f32[8,256,64]{1,2,0:T(8,128)S(1)} fusion(f32[8,256,1024]{1,2,0:T(8,128)} %bitcast.166, f32[8,1024,64]{1,2,0:T(8,128)S(1)} %fusion.8), kind=kOutput, calls=%fused_computation.197 | convolution fusion | flops 1610612736 | bytes 11010048 | tf_op jit(solution)/shard_map/jvp()/while/body/eval_jaxpr/hif,hfd->hid/dot_general | solution.py:122
  297.4 1.1 fusion.41
  298.5 10.2 %fusion.119 = bf16[8,1,1024]{2,1,0:T(2,128)(2,1)S(1)} fusion(f32[8,256,1024]{1,2,0:T(8,128)} %bitcast.167, f32[8,256,1]{1,0,2:T(8,128)S(1)} %get-tuple-element.399), kind=kOutput, calls=%fused_computation.187 | convolution fusion | flops 25165824 | bytes 8413184 | tf_op jit(solution)/shard_map/transpose(jvp())/while/body/eval_jaxpr/hif,hf->hi/dot_general | solution.py:128
  309.9 9.3 %multiply_add_fusion = f32[8,256,1024]{2,1,0:T(8,128)} fusion(f32[8,1024]{1,0:T(8,128)S(1)} %fusion.68, f32[8,256]{1,0:T(8,128)S(1)} %get-tuple-element.400, f32[8,1024,64]{1,2,0:T(8,128)S(1)} %fusion.8, f32[8,256]{1,0:T(8,128)S(1)} %get-tuple-element.397, f32[256,512]{0,1:T(8,128)S(1)} %copy.59), kind=kOutput, calls=%fused_computation.6 | convolution fusion | flops 1614938112 | bytes 11059200 | tf_op jit(solution)/shard_map/transpose(jvp())/while/body/eval_jaxpr/hif,hfd->hid/dot_general | solution.py:122
  319.2 9.2 %copy.66 = f32[8,256,1024]{1,2,0:T(8,128)} copy(f32[8,256,1024]{2,1,0:T(8,128)} %multiply_add_fusion) | data formatting | bytes 16777216 | tf_op jit(solution)/shard_map/transpose(jvp())/while/body/eval_jaxpr/hif,hfd->hid/add_any | solution.py:122
  328.4 2.9 add_multiply_fusion
  331.3 8.9 %multiply_reduce_fusion.5 = (f32[8,256,32]{1,2,0:T(8,128)S(1)}, f32[8,256,32]{1,2,0:T(8,128)S(1)}) fusion(f32[8,256,32,32]{1,3,2,0:T(8,128)} %bitcast.172, f32[8,256,32]{1,2,0:T(8,128)S(1)} %get-tuple-element.401, f32[8,256,1024]{1,2,0:T(8,128)} %copy.66), kind=kLoop, calls=%fused_computation.5 | loop fusion | flops 8257536 | bytes 17563648 | tf_op jit(solution)/shard_map/transpose(jvp())/while/body/eval_jaxpr/reduce_sum | solution.py:106
  340.2 1.4 fusion.44
  342.2 1.3 fusion.40
  343.6 1.8 copy.77
  345.4 2.5 all-gather.1
  347.9 9.4 %all_gather.63 = bf16[4,8,1024]{2,1,0:T(8,128)(2,1)S(1)} all-gather(bf16[1,8,1024]{2,1,0:T(8,128)(2,1)S(1)} %fusion.93), channel_id=1, replica_groups=mesh['seq_0'=4,'seq_1'=4,'seq_2'=2,'head'=4] {'seq_1'}, dimensions={0}, use_global_device_ids=true | all-gather | bytes 81920 | tf_op jit(solution)/shard_map/all_gather | solution.py:65
  358.0 9.7 %all_gather.64 = bf16[4,8,1024]{2,1,0:T(8,128)(2,1)} all-gather(bf16[1,8,1024]{2,1,0:T(8,128)(2,1)S(1)} %fusion.90), channel_id=1, replica_groups=mesh['seq_0'=4,'seq_1'=4,'seq_2'=2,'head'=4] {'seq_0'}, dimensions={0}, use_global_device_ids=true | all-gather | bytes 81920 | tf_op jit(solution)/shard_map/all_gather | solution.py:65
  367.7 3.0 fusion.129
  370.7 5.9 %fusion.18 = f32[8,1024,64]{1,2,0:T(8,128)S(1)} fusion(f32[8,1024,64]{1,2,0:T(8,128)} %param.18, bf16[4,8,1024,64]{2,3,1,0:T(8,128)(2,1)} %all-gather.16.cloned.1.call-done, pred[]{:T(512)S(6)} %lt.44, pred[]{:T(512)S(6)} %lt.45, pred[]{:T(512)S(6)} %lt.40, pred[]{:T(512)S(6)} %lt.36, pred[]{:T(512)S(6)} %lt.43, pred[]{:T(512)S(6)} %lt.42, pred[]{:T(512)S(6)} %lt.41, ...), kind=kLoop, calls=%fused_computation.42 | loop fusion | flops 15728640 | bytes 14680074 | tf_op jit(solution)/shard_map/add | solution.py:258
  376.6 9.5 %fusion.130 = f32[8,256,64]{1,2,0:T(8,128)} fusion(f32[8,256,1024]{1,2,0:T(8,128)} %bitcast.170, f32[8,1024,64]{1,2,0:T(8,128)S(1)} %fusion.18), kind=kOutput, calls=%fused_computation.199 | convolution fusion | flops 1610612736 | bytes 11010048 | tf_op jit(solution)/shard_map/transpose(jvp())/while/body/eval_jaxpr/hjf,hjd->hfd/dot_general | solution.py:173
  386.1 1.1 pad_maximum_fusion
  388.2 7.5 %broadcast_add_fusion = f32[8,256,1024]{2,1,0:T(8,128)} fusion(f32[8,1024]{1,0:T(8,128)S(1)} %fusion.81, bf16[8,256,64]{1,2,0:T(8,128)(2,1)S(1)} %bitcast.179, f32[8,1024,64]{1,2,0:T(8,128)} %copy-done.6), kind=kOutput, calls=%fused_computation.7 | convolution fusion | flops 1612709888 | bytes 10780672 | tf_op jit(solution)/shard_map/transpose(jvp())/while/body/eval_jaxpr/hjf,hjd->hfd/dot_general | solution.py:173
  395.7 9.1 %copy.70 = f32[8,256,1024]{1,2,0:T(8,128)} copy(f32[8,256,1024]{2,1,0:T(8,128)} %broadcast_add_fusion) | data formatting | bytes 16777216 | tf_op jit(solution)/shard_map/transpose(jvp())/while/body/eval_jaxpr/hjf,hjd->hfd/add_any | solution.py:173
  404.8 9.0 %multiply_reduce_fusion = (f32[8,256,32]{1,2,0:T(8,128)S(1)}, f32[8,256,32]{1,2,0:T(8,128)S(1)}) fusion(f32[8,256,32]{1,2,0:T(8,128)S(1)} %get-tuple-element.403, f32[8,256,1024]{1,2,0:T(8,128)} %copy.70, f32[8,256,32,32]{1,3,2,0:T(8,128)} %bitcast.173), kind=kLoop, calls=%fused_computation | loop fusion | flops 8257536 | bytes 17563648 | tf_op jit(solution)/shard_map/transpose(jvp())/while/body/eval_jaxpr/reduce_sum | solution.py:106
  413.8 2.0 fusion.42
  419.3 4.5 convolution_add_fusion.1
  423.8 2.3 fusion.38
  427.0 3.0 fusion.1
  430.0 1.1 copy.109
  431.1 4.0 all-to-all-start.1
  435.0 62.0 %all-reduce.2.cloned.1.call-done = bf16[532480]{0:T(1024)(128)(2,1)} async-done(((bf16[532480]{0:T(1024)(128)(2,1)}), bf16[532480]{0:T(1024)(128)(2,1)}) %all-reduce.2.cloned.1.call-update) | async-done | bytes 1064976 | tf_op jit(solution)/shard_map/psum | solution.py:95
  497.1 2.7 slice_convert_fusion
  501.1 4.3 reshape.415
  505.5 5.9 %add.295 = f32[8,1024,64]{2,1,0:T(8,128)} add(f32[8,1024,64]{2,1,0:T(8,128)} %copy.76, f32[8,1024,64]{2,1,0:T(8,128)} %reshape.415) | non-fusion elementwise | flops 524288 | bytes 6291456 | tf_op jit(solution)/shard_map/add | solution.py:275
  511.3 3.8 copy.80
  (98 shorter events, 14.9 us)
Async XLA Ops:
  7.2 27.6 %copy-start = (bf16[2048,512]{1,0:T(8,128)(2,1)S(1)}, bf16[2048,512]{1,0:T(8,128)(2,1)}, u32[]{:S(2)}) copy-start(bf16[2048,512]{1,0:T(8,128)(2,1)} %param.11) | copy-start | bytes 6291460
  7.2 7.1 %copy-start.23 = (bf16[256,512]{1,0:T(8,128)(2,1)S(1)}, bf16[256,512]{1,0:T(8,128)(2,1)}, u32[]{:S(2)}) copy-start(bf16[256,512]{1,0:T(8,128)(2,1)} %param.17) | copy-start | bytes 786436
  9.5 19.2 %all-to-all-start = ((bf16[4,256,512]{1,2,0:T(8,128)(2,1)}), bf16[4,256,512]{1,2,0:T(8,128)(2,1)}, u32[]{:S(2)}, u32[]{:S(2)}) async-start(bf16[4,256,512]{1,2,0:T(8,128)(2,1)} %broadcast_in_dim.136), calls=%async_computation | async-start | bytes 2097152 | tf_op jit(solution)/shard_map/all_to_all | solution.py:23
  14.3 99.9 %all-gather.18.cloned.1.call-start = ((), (), s32[]{:S(2)}) async-start(), calls=%async_computation.7 | async-start | bytes 3145728 | tf_op jit(solution)/shard_map/all_gather | solution.py:44
  34.8 3.2 copy-start.17
  38.0 0.7 copy-start.10
  38.3 3.6 copy-start.8
  39.0 2.9 copy-start.11
  55.1 0.6 copy-start.22
  66.2 0.6 copy-start.19
  86.1 45.9 %all-gather.20.cloned.1.call-start = ((), (), s32[]{:S(2)}) async-start(), calls=%async_computation.8 | async-start | bytes 3145728 | tf_op jit(solution)/shard_map/all_gather | solution.py:65
  91.5 4.4 copy-start.1
  114.2 68.7 %all-gather.10.cloned.1.call-start = ((), (), s32[]{:S(2)}) async-start(), calls=%async_computation.2 | async-start | bytes 5242880 | tf_op jit(solution)/shard_map/all_gather | solution.py:44
  117.2 115.8 %all-gather.14.cloned.1.call-start = ((), (), s32[]{:S(2)}) async-start(), calls=%async_computation.4 | async-start | bytes 5242880 | tf_op jit(solution)/shard_map/all_gather | solution.py:65
  135.0 148.0 %all-gather.12.cloned.1.call-start = ((), (), s32[]{:S(2)}) async-start(), calls=%async_computation.3 | async-start | bytes 5242880 | tf_op jit(solution)/shard_map/all_gather | solution.py:44
  187.0 183.7 %all-gather.16.cloned.1.call-start = ((), (), s32[]{:S(2)}) async-start(), calls=%async_computation.5 | async-start | bytes 5242880 | tf_op jit(solution)/shard_map/all_gather | solution.py:65
  237.1 260.0 %all-reduce.2.cloned.1.call-start = ((), (), s32[]{:S(2)}) async-start(), calls=%async_computation.6 | async-start | bytes 2129920 | tf_op jit(solution)/shard_map/psum | solution.py:95
  288.9 8.5 %copy-start.2 = (f32[8,256,256]{1,2,0:T(8,128)S(1)}, f32[8,256,256]{1,2,0:T(8,128)}, u32[]{:S(2)}) copy-start(f32[8,256,256]{1,2,0:T(8,128)} %get-tuple-element.406) | copy-start | bytes 6291460
  331.2 8.9 %copy-start.4 = (f32[8,256,256]{1,2,0:T(8,128)}, f32[8,256,256]{1,2,0:T(8,128)S(1)}, u32[]{:S(2)}) copy-start(f32[8,256,256]{1,2,0:T(8,128)S(1)} %add_multiply_fusion) | copy-start | bytes 6291460
  340.2 1.4 copy-start.16
  340.2 2.0 copy-start.12
  357.3 0.6 copy-start.18
  376.6 9.5 %copy-start.6 = (f32[8,1024,64]{1,2,0:T(8,128)}, f32[8,1024,64]{1,2,0:T(8,128)S(1)}, u32[]{:S(2)}) copy-start(f32[8,1024,64]{1,2,0:T(8,128)S(1)} %fusion.18) | copy-start | bytes 6291460
  376.6 9.5 %copy-start.7 = (bf16[524288]{0:T(1024)(128)(2,1)S(1)}, bf16[524288]{0:T(1024)(128)(2,1)}, u32[]{:S(2)}) copy-start(bf16[524288]{0:T(1024)(128)(2,1)} %reshape.397) | copy-start | bytes 3145732
  376.6 9.5 %copy-start.25 = (bf16[1,8,8,128]{3,1,2,0:T(8,128)(2,1)S(1)}, bf16[1,8,8,128]{3,1,2,0:T(8,128)(2,1)}, u32[]{:S(2)}) copy-start(bf16[1,8,8,128]{3,1,2,0:T(8,128)(2,1)} %copy.111) | copy-start | bytes 49156
  404.8 9.0 %copy-start.5 = (f32[8,256,256]{1,2,0:T(8,128)S(1)}, f32[8,256,256]{1,2,0:T(8,128)}, u32[]{:S(2)}) copy-start(f32[8,256,256]{1,2,0:T(8,128)} %copy-done.4) | copy-start | bytes 6291460
  404.8 9.0 %copy-start.14 = (f32[8,256,32]{1,2,0:T(8,128)S(1)}, f32[8,256,32]{1,2,0:T(8,128)}, u32[]{:S(2)}) copy-start(f32[8,256,32]{1,2,0:T(8,128)} %get-tuple-element.389) | copy-start | bytes 786436
  404.8 9.0 %copy-start.15 = (f32[8,256,32]{1,2,0:T(8,128)S(1)}, f32[8,256,32]{1,2,0:T(8,128)}, u32[]{:S(2)}) copy-start(f32[8,256,32]{1,2,0:T(8,128)} %get-tuple-element.391) | copy-start | bytes 786436
  413.8 2.1 copy-start.13
  413.8 3.3 copy-start.9
  419.3 4.5 copy-start.3
  419.3 4.5 copy-start.20
  419.3 4.5 copy-start.21
  431.1 84.0 %all-to-all-start.1 = ((bf16[4,256,512]{2,1,0:T(8,128)(2,1)}), bf16[4,256,512]{2,1,0:T(8,128)(2,1)S(1)}, u32[]{:S(2)}, u32[]{:S(2)}) async-start(bf16[4,256,512]{2,1,0:T(8,128)(2,1)} %bitcast.180), calls=%async_computation.1 | async-start | bytes 2097152 | tf_op jit(solution)/shard_map/all_to_all | solution.py:87
  435.0 65.5 %copy-start.24 = (f32[8,1024]{1,0:T(8,128)S(1)}, f32[8,1024]{1,0:T(8,128)}, u32[]{:S(2)}) copy-start(f32[8,1024]{1,0:T(8,128)} %param.19) | copy-start | bytes 98308
Sparse Core Ops, SparseCore 0:
  86.2 17.6 all-gather.17
  114.3 17.6 all-gather.19
  133.7 49.1 all-gather.9
  184.4 48.5 all-gather.13
  234.6 48.3 all-gather.11
  284.5 48.5 all-gather.15
  387.4 109.6 all-reduce.1
where the time goes:
time: 526 us; the launch traced here: 523 us
  waiting for transfers between devices  212 us (40%)
  matrix products  128 us (24%)
  other arithmetic  64.2 us (12%)
  local copies, waits for them, and re-layouts  49.9 us (9%)
  blocking collectives  45.9 us (9%)
  between operations  14.9 us (3%)
  starting transfers between devices  9.05 us (2%)
    all_gather x3, waiting for transfers between devices, prefix_by_axis(): lax.all_gather(part.astype(kind), axis)  74.4 us
    psum x1, waiting for transfers between devices, packed_total(): subtotal = lax.psum(jnp.concatenate([a.ravel() for a in arrays]), axis)  62 us
    all_gather x3, waiting for transfers between devices, carried_in(): lax.all_gather(part.astype(kind), axis)  60.7 us
    dot_general x3, matrix products, attend_block(): jnp.einsum('hif,hfd->hid', feat_query, value_state, precision=HIGHEST_PRE...  36 us
    dot_general x3, matrix products, add_block(): jnp.einsum('hjf,hjd->hfd', feat_key, value_block, precision=HIGHEST_PRECI...  25.8 us
    all_gather x3, blocking collectives, prefix_by_axis(): lax.all_gather(part.astype(kind), axis)  24.2 us
    reduce_sum x3, other arithmetic, square_features(): outer_prod = sketched[:, :, :, None] * sketched[:, :, None, :]  23.5 us
    all_gather x3, blocking collectives, carried_in(): lax.all_gather(part.astype(kind), axis)  21.7 us
  transfers between devices with their start and end apart: 9, of which 6 were waited for; matrix products, arithmetic and copies ran while one was open for 36% of the time, Pallas kernels for 0%

commit v1 on v0

v1 whole, which is shorter than its diff:
```python
import jax
import jax.numpy as jnp
from jax import lax
from jax.experimental import pallas as pl
from jax.experimental.pallas import tpu as pltpu
from jax.sharding import Mesh
from jax.sharding import PartitionSpec as P

SEQ = ("seq_0", "seq_1", "seq_2")
MESH = pl.DeviceIdType.MESH
F32 = jnp.float32
BF = jnp.bfloat16

SK = 32
NS = 17
NF = NS * SK
NP = 640
TOK = 256
CT = 512
CH = 16
ROWS = 80
OWN = 14
WIRE = OWN * ROWS
ZROW = 2 * NF


def nn(a, b):
    return lax.dot_general(a, b, (((1,), (0,)), ((), ())), preferred_element_type=F32)


def nt(a, b):
    return lax.dot_general(a, b, (((1,), (1,)), ((), ())), preferred_element_type=F32)


def kernel(
    x_hbm, wq_hbm, wk_hbm, wv_hbm, g_hbm, ps_hbm, pn_hbm, da_hbm, de_hbm, dn_hbm,
    oi_hbm, oq_hbm, ok_hbm, ov_hbm, os_hbm, on_hbm,
    xg, w, acc, qkv, xsend, ga, gt, psv, pnv, dev, dnv, dps, dpn,
    bd, bdh, bdl, bdt, lrt, skt, skb, stok, feat, vtm, vtok, dext, fold, stk, fsel,
    yloc, gtr, scr, dmat, wmat, yv, tmp, zst, zpad, dfe, dst, dvt, sext, sextt,
    wire, inb, outb, res, totb, tot, dtok, dall, acc2, rsend, rrecv, oin,
    loc, ag_s, ag_r, ex_s, ex_r, a_s, a_r, b_s, b_r, t_s, t_r, rs_s, rs_r,
):
    y = lax.axis_index("seq_0")
    z = lax.axis_index("seq_1")
    c = lax.axis_index("seq_2")
    x = lax.axis_index("head")
    m = y * 4 + z
    oc = 1 - c
    right, left, far = lax.rem(x + 1, 4), lax.rem(x + 3, 4), lax.rem(x + 2, 4)

    def rc(src, dst_, ss, rs, **where):
        return pltpu.make_async_remote_copy(
            src_ref=src, dst_ref=dst_, send_sem=ss, recv_sem=rs,
            device_id=where, device_id_type=MESH,
        )

    own_cols = pl.ds(pl.multiple_of(c * 256, 256), 256)
    oth_cols = pl.ds(pl.multiple_of(oc * 256, 256), 256)

    lx = [
        pltpu.make_async_copy(x_hbm.at[:, 256 * k : 256 * k + 256], xg.at[2 * x + k], loc.at[k])
        for k in range(2)
    ]
    lw = [
        pltpu.make_async_copy(src, w.at[t], loc.at[2 + t])
        for t, src in enumerate((wq_hbm, wk_hbm, wv_hbm))
    ]
    lg = pltpu.make_async_copy(g_hbm, gt, loc.at[5])
    la = pltpu.make_async_copy(da_hbm.at[:, own_cols], ga.at[c], loc.at[6])
    ln = pltpu.make_async_copy(pn_hbm, pnv, loc.at[7])
    lp = pltpu.make_async_copy(ps_hbm.at[pl.ds(4 * c, 4)], psv, loc.at[8])
    le = pltpu.make_async_copy(de_hbm, dev, loc.at[9])
    lm = pltpu.make_async_copy(dn_hbm, dnv, loc.at[10])
    for copy in (lx[0], lx[1], lw[1], lw[2], lw[0], lg, la, ln, lp, le, lm):
        copy.start()

    bar = pltpu.get_barrier_semaphore()
    for peer in (right, left):
        pl.semaphore_signal(bar, inc=1, device_id={"head": peer}, device_id_type=MESH)
    pl.semaphore_signal(bar, inc=1, device_id={"seq_2": oc}, device_id_type=MESH)

    def greet(d, _):
        r = lax.rem(m + d, CH)
        pl.semaphore_signal(
            bar, inc=1, device_id={"seq_0": r // 4, "seq_1": lax.rem(r, 4)}, device_id_type=MESH
        )
        return 0

    lax.fori_loop(1, CH, greet, 0)
    pl.semaphore_wait(bar, 18)

    def slab(src, k, peer, i):
        ref = xg.at[2 * src + k]
        return rc(ref, ref, ag_s.at[i], ag_r.at[i], head=peer)

    ag = [
        slab(x, 0, right, 0), slab(x, 1, left, 1), slab(x, 1, right, 2), slab(x, 0, left, 3),
        slab(left, 0, right, 4), slab(right, 1, left, 5),
    ]
    lx[0].wait()
    lx[1].wait()
    for i in range(4):
        ag[i].start()
    cga = rc(da_hbm.at[:, oth_cols], ga.at[c], ex_s.at[0], ex_r.at[0], seq_2=oc)
    cga.start()

    lg.wait()
    bd[...] = jnp.zeros((256, 256), F32)
    lane128 = lax.broadcasted_iota(jnp.int32, (SK, 128), 1) // 64
    for lr in range(2):
        wide = jnp.concatenate([gt[lr], gt[lr]], axis=1)
        for h in range(4):
            row = lr * 128 + h * SK
            col = 128 * (h // 2)
            bd[row : row + SK, col : col + 128] = jnp.where(lane128 == h % 2, wide, 0.0)
    bdh[...] = bd[...].astype(BF)
    bdl[...] = (bd[...] - bdh[...].astype(F32)).astype(BF)
    bdt[0] = jnp.transpose(bd[...]).astype(BF)
    bdt[1] = (jnp.transpose(bd[...]) - bdt[0].astype(F32)).astype(BF)

    for t in range(3):
        lw[(1, 2, 0)[t]].wait()

    def project(src, first):
        for t in range(3):
            out = nn(xg[2 * src], w[t, pl.ds(pl.multiple_of(src * 512, 512), 256), :])
            out = out + nn(xg[2 * src + 1], w[t, pl.ds(pl.multiple_of(src * 512 + 256, 256), 256), :])
            if first:
                acc[t] = out
            else:
                acc[t] += out

    project(x, True)
    ag[0].wait_recv()
    ag[4].start()
    ag[1].wait_recv()
    ag[5].start()

    def build(i, _):
        f = lax.broadcasted_iota(jnp.int32, (SK, 1024), 1)
        fi, fj = f // SK, lax.rem(f, SK)
        a = lax.broadcasted_iota(jnp.int32, (SK, 1024), 0)
        b = lax.rem(a + i, SK)
        hit = ((fi == a) & (fj == b)) | ((fi == b) & (fj == a))
        value = jnp.where(i == 16, 0.5, 1.0)
        keep = jnp.where(i < NS, value, 0.0)
        fsel[pl.ds(pl.multiple_of(i * SK, SK), SK), :] = jnp.where(hit, keep, 0.0).astype(BF)
        return 0

    lax.fori_loop(0, NP // SK, build, 0)
    for h in range(4):
        for q in range(2):
            feat[q, h, NF:NP, :] = jnp.zeros((NP - NF, CT), BF)
    zpad[...] = jnp.zeros((128, NP), F32)
    tmp[...] = jnp.zeros((NP, 128), F32)
    dext[...] = jnp.zeros(dext.shape, BF)
    stk[...] = jnp.zeros(stk.shape, BF)
    zst[...] = jnp.zeros((SK, 128), F32)
    vtm[...] = jnp.zeros(vtm.shape, BF)
    sext[...] = jnp.zeros(sext.shape, F32)

    ag[2].wait_recv()
    project(left, False)
    ag[3].wait_recv()
    project(right, False)
    ag[4].wait_recv()
    ag[5].wait_recv()

    cqkv = {}
    for t in (1, 2, 0):
        dst_ref = qkv.at[t, c]
        cqkv[t] = rc(xsend.at[t], dst_ref, ex_s.at[1 + t], ex_r.at[1 + t], seq_2=oc)
        for cols, target in ((oth_cols, None), (own_cols, c)):
            out = acc[t, :, cols] + nn(
                xg[2 * far], w[t, pl.ds(pl.multiple_of(far * 512, 512), 256), cols]
            )
            out = out + nn(
                xg[2 * far + 1], w[t, pl.ds(pl.multiple_of(far * 512 + 256, 256), 256), cols]
            )
            if target is None:
                xsend[t] = out.astype(BF)
                cqkv[t].start()
            else:
                qkv[t, target] = out.astype(BF)

    scale = SK ** (-0.5)

    def sketch(t):
        for k in range(2):
            part = slice(256 * k, 256 * k + 256)
            lrt[t, :, part] = nt(bdh[...], qkv[t, k]) + nt(bdl[...], qkv[t, k])
            tok = nt(qkv[t, k], bdh[...]) + nt(qkv[t, k], bdl[...])
            stok[t, part, :] = (tok[:, :128] * tok[:, 128:] * scale).astype(BF)
        skt[t] = lrt[t, :128, :] * lrt[t, 128:, :] * scale
        skb[t] = skt[t].astype(BF)

        def one(h, _):
            s = skt[t, pl.ds(pl.multiple_of(h * SK, SK), SK), :]
            for i in range(NS):
                other = s if i == 0 else pltpu.roll(s, SK - i, 0)
                feat[t, h, SK * i : SK * i + SK, :] = (s * other).astype(BF)
            return 0

        lax.fori_loop(0, 4, one, 0)

    lane256 = lax.broadcasted_iota(jnp.int32, (CT, 256), 1)

    def pack_z(total):
        tmp[0:NF, :] = total
        zt = jnp.transpose(tmp[...])
        for j in range(5):
            zst[4 * j : 4 * j + 4, :] = zt[0:4, 128 * j : 128 * j + 128]
        wire[ZROW:WIRE, :] = zst[...].astype(BF)

    cqkv[1].wait_recv()
    sketch(1)
    cqkv[2].wait_recv()
    for p in range(2):
        for k in range(2):
            vtok[p, 256 * k : 256 * k + 256, 0:128] = qkv[2, k, :, 128 * p : 128 * p + 128]
        vtok[p, :, 128:256] = jnp.ones((CT, 128), BF)
    ztot = None
    for p in range(2):
        out = None
        for hh in range(2):
            h = 2 * p + hh
            keep = (lane256 // 64 == hh) | (lane256 == 128 + h)
            vm = jnp.where(keep, vtok[p].astype(F32), 0.0).astype(BF)
            part = nn(feat[1, h, 0:NF, :], vm)
            out = part if out is None else out + part
        wire[NF * p : NF * p + NF, :] = out[:, 0:128].astype(BF)
        ztot = out[:, 128:256] if ztot is None else ztot + out[:, 128:256]
    pack_z(ztot)

    def scan_send(n):
        def one(d, _):
            r = lax.rem(m + d, CH)

            @pl.when(r < OWN)
            def _():
                rc(
                    wire.at[pl.ds(pl.multiple_of(r * ROWS, ROWS), ROWS)], inb.at[n, m],
                    a_s.at[n, r], a_r.at[n, m], seq_0=r // 4, seq_1=lax.rem(r, 4),
                ).start()

            return 0

        lax.fori_loop(1, CH, one, 0)

        @pl.when(m < OWN)
        def _():
            inb[n, m] = wire[pl.ds(pl.multiple_of(m * ROWS, ROWS), ROWS), :]

    def a_copy(n, r):
        return rc(
            wire.at[pl.ds(0, ROWS)], inb.at[n, r], a_s.at[n, r], a_r.at[n, r],
            seq_0=r // 4, seq_1=lax.rem(r, 4),
        )

    def mine(ref):
        return ref.at[pl.ds(pl.multiple_of(m * ROWS, ROWS), ROWS)]

    def b_copy(n, r):
        return rc(
            outb.at[n, r], mine(res.at[n]), b_s.at[n, r], b_r.at[n, m],
            seq_0=r // 4, seq_1=lax.rem(r, 4),
        )

    def t_copy(r):
        return rc(
            totb, mine(tot.at[c]), t_s.at[r], t_r.at[m], seq_0=r // 4, seq_1=lax.rem(r, 4)
        )

    def scan_own(n, reverse):
        @pl.when(m < OWN)
        def _():
            def one(i, running):
                r = CH - 1 - i if reverse else i

                @pl.when(r != m)
                def _():
                    a_copy(n, r).wait_recv()

                outb[n, r] = running.astype(BF)

                @pl.when(r != m)
                def _():
                    b_copy(n, r).start()

                @pl.when(r == m)
                def _():
                    res[n, pl.ds(pl.multiple_of(m * ROWS, ROWS), ROWS), :] = running.astype(BF)

                return running + inb[n, r].astype(F32)

            total = lax.fori_loop(0, CH, one, jnp.zeros((ROWS, 128), F32))
            if reverse:
                totb[...] = total.astype(BF)
                tot[c, pl.ds(pl.multiple_of(m * ROWS, ROWS), ROWS), :] = total.astype(BF)

                def share(d, _):
                    t_copy(lax.rem(m + d, CH)).start()
                    return 0

                lax.fori_loop(1, CH, share, 0)

    def from_owners(make):
        def one(s, _):
            @pl.when(s != m)
            def _():
                make(s).wait_recv()

            return 0

        lax.fori_loop(0, OWN, one, 0)

    def b_in(n, s):
        block = res.at[n, pl.ds(pl.multiple_of(s * ROWS, ROWS), ROWS)]
        return rc(outb.at[n, s], block, b_s.at[n, s], b_r.at[n, s], seq_0=s // 4, seq_1=lax.rem(s, 4))

    def t_in(s):
        block = tot.at[c, pl.ds(pl.multiple_of(s * ROWS, ROWS), ROWS)]
        return rc(totb, block, t_s.at[s], t_r.at[s], seq_0=s // 4, seq_1=lax.rem(s, 4))

    def sends_done(n):
        def one(d, _):
            r = lax.rem(m + d, CH)

            @pl.when(r < OWN)
            def _():
                a_copy(n, r).wait_send()

            @pl.when(m < OWN)
            def _():
                b_copy(n, r).wait_send()
                if n == 1:
                    t_copy(r).wait_send()

            return 0

        lax.fori_loop(1, CH, one, 0)

    def fold_in(state, norm):
        stk[0:256, :] = state
        pick = jnp.where(c == 0, norm[0:4, :], norm[4:8, :])
        stk[256:272, :] = jnp.concatenate([pick, jnp.zeros((12, 1024), F32)], axis=0).astype(BF)
        fold[...] = nt(fsel[...], stk[...])

    row_w = lax.broadcasted_iota(jnp.int32, (NF, 128), 0)
    weight = jnp.where((row_w < SK) | (row_w >= 16 * SK), 1.0, 2.0)

    def unpack(n):
        zst[...] = res[n, ZROW:WIRE, :].astype(F32)
        for j in range(5):
            zpad[0:4, 128 * j : 128 * j + 128] = zst[4 * j : 4 * j + 4, :]
        zc = jnp.transpose(zpad[...])[0:NF, :] * weight + fold[0:NF, 256:384]
        for p in range(2):
            part = res[n, NF * p : NF * p + NF, :].astype(F32)
            sext[p, 0:NF, 0:128] = part * weight + fold[0:NF, 128 * p : 128 * p + 128]
            sext[p, 0:NF, 128:256] = zc
            sextt[p] = jnp.transpose(sext[p])[0:144, :].astype(BF)

    scan_send(0)

    lp.wait()
    ln.wait()
    fold_in(psv[...].reshape(256, 1024).astype(BF), pnv)
    cqkv[0].wait_recv()
    sketch(0)

    scan_own(0, False)

    la.wait()
    cga.wait_recv()
    for k in range(2):
        part = slice(256 * k, 256 * k + 256)
        gtr[:, part] = jnp.transpose(ga[k].astype(F32))
        vt = jnp.transpose(qkv[2, k].astype(F32)).astype(BF)
        for h in range(4):
            vtm[h, 64 * (h % 2) : 64 * (h % 2) + 64, part] = vt[64 * h : 64 * h + 64, :]
    row16 = lax.broadcasted_iota(jnp.int32, (16, CT), 0)
    for h in range(4):
        vtm[h, 128:144, :] = jnp.where(row16 == h, 1.0, 0.0).astype(BF)

    diag = lax.broadcasted_iota(jnp.int32, (256, 256), 0) <= lax.broadcasted_iota(
        jnp.int32, (256, 256), 1
    )
    lane_k = lax.broadcasted_iota(jnp.int32, (256, 128), 1) // SK

    def scores(h, _):
        for jb in range(2):
            keys = jnp.where(lane_k == h, stok[1, 256 * jb : 256 * jb + 256, :].astype(F32), 0.0)
            keys = keys.astype(BF)
            for ib in range(jb, 2):
                d = nn(keys, skb[0, :, 256 * ib : 256 * ib + 256])
                if ib == jb:
                    d = jnp.where(diag, d, 0.0)
                at = (h, slice(256 * jb, 256 * jb + 256), slice(256 * ib, 256 * ib + 256))
                scr[at] = (d * d).astype(BF)
                dmat[at] = (d + d).astype(BF)
        yloc[h, :, 0:256] = nn(vtm[h, 0:144, 0:256], scr[h, 0:256, 0:256])
        yloc[h, :, 256:512] = nn(vtm[h, 0:144, :], scr[h, :, 256:512])
        return 0

    lax.fori_loop(0, 4, scores, 0)

    from_owners(lambda s: b_in(0, s))
    unpack(0)
    ztot = None
    for p in range(2):
        out = None
        for hh in range(2):
            h = 2 * p + hh
            yv[...] = nn(sextt[p], feat[0, h]) + yloc[h]
            num = yv[64 * hh : 64 * hh + 64, :]
            inv = 1.0 / (1.0 + yv[128 + h : 129 + h, :])
            g = gtr[64 * h : 64 * h + 64, :]
            dden = -jnp.sum(g * num, axis=0, keepdims=True) * inv * inv
            dext[h, 64 * hh : 64 * hh + 64, :] = (g * inv).astype(BF)
            dext[h, 128:144, :] = jnp.where(row16 == h, dden, 0.0).astype(BF)
            part = nt(feat[0, h, 0:NF, :], dext[h])
            out = part if out is None else out + part
        if p == 0:

            def first_sent(d, _):
                r = lax.rem(m + d, CH)

                @pl.when(r < OWN)
                def _():
                    a_copy(0, r).wait_send()

                return 0

            lax.fori_loop(1, CH, first_sent, 0)
        wire[NF * p : NF * p + NF, :] = out[:, 0:128].astype(BF)
        ztot = out[:, 128:256] if ztot is None else ztot + out[:, 128:256]
    pack_z(ztot)
    scan_send(1)

    def feature_grad(t, h, extra):
        s = skt[t, pl.ds(pl.multiple_of(h * SK, SK), SK), :]
        here = 2.0 * s * dfe[0:SK, :]
        for i in range(1, NS):
            d = dfe[SK * i : SK * i + SK, :]
            here = here + d * pltpu.roll(s, SK - i, 0) + pltpu.roll(d * s, i, 0)
        dst[t, pl.ds(pl.multiple_of(h * SK, SK), SK), :] = here + extra

    def local_grads(h, _):
        p = h // 2
        for jb in range(2):
            for ib in range(jb, 2):
                at = (h, slice(256 * jb, 256 * jb + 256), slice(256 * ib, 256 * ib + 256))
                ds = nn(vtok[p, 256 * jb : 256 * jb + 256, :], dext[h, :, 256 * ib : 256 * ib + 256])
                wmat[at] = (dmat[at].astype(F32) * ds).astype(BF)
        sk_rows = pl.ds(pl.multiple_of(h * SK, SK), SK)
        d_rows = pl.ds(pl.multiple_of(64 * lax.rem(h, 2), 64), 64)
        v_rows = pl.ds(pl.multiple_of(64 * h, 64), 64)
        dst[0, sk_rows, 0:256] = nn(skb[1, sk_rows, 0:256], wmat[h, 0:256, 0:256])
        dst[0, sk_rows, 256:512] = nn(skb[1, sk_rows, :], wmat[h, :, 256:512])
        dst[1, sk_rows, 0:256] = nt(skb[0, sk_rows, :], wmat[h, 0:256, :])
        dst[1, sk_rows, 256:512] = nt(skb[0, sk_rows, 256:512], wmat[h, 256:512, 256:512])
        dvt[v_rows, 0:256] = nt(dext[h, d_rows, :], scr[h, 0:256, :])
        dvt[v_rows, 256:512] = nt(dext[h, d_rows, 256:512], scr[h, 256:512, 256:512])
        return 0

    def through_sketch(t):
        lt, rt = lrt[t, :128, :], lrt[t, 128:, :]
        ds = dst[t] * scale
        dlr = jnp.concatenate([ds * rt, ds * lt], axis=0).astype(BF)
        return nn(bdt[0], dlr) + nn(bdt[1], dlr)

    own_rows = pl.ds(pl.multiple_of(c * 256, 256), 256)
    oth_rows = pl.ds(pl.multiple_of(oc * 256, 256), 256)

    def hand_over(t, grad):
        dtok[t] = jnp.transpose(grad).astype(BF)
        copy = rc(dtok.at[t, oth_rows], dall.at[t, c], ex_s.at[4 + t], ex_r.at[4 + t], seq_2=oc)
        copy.start()
        dall[t, c] = dtok[t, own_rows, :]
        return copy

    lax.fori_loop(0, 4, local_grads, 0)

    def grad_q(h, _):
        dfe[...] = nn(sext[h // 2, 0:NF, :].astype(BF), dext[h])
        feature_grad(0, h, dst[0, pl.ds(pl.multiple_of(h * SK, SK), SK), :])
        return 0

    lax.fori_loop(0, 4, grad_q, 0)
    copy_q = hand_over(0, through_sketch(0))

    scan_own(1, True)

    le.wait()
    lm.wait()
    fold_in(dev[pl.ds(4 * c, 4)].reshape(256, 1024).astype(BF), dnv)
    copy_q.wait_recv()

    def store(t, ref, base):
        made = [
            pltpu.make_async_copy(dall.at[t, k], ref.at[:, 256 * k : 256 * k + 256], loc.at[base + k])
            for k in range(2)
        ]
        for one in made:
            one.start()
        return made

    stores = store(0, oq_hbm, 11)

    def pull(t, b):
        out = None
        for k in range(2):
            part = nt(dall[t, k], w[t, pl.ds(pl.multiple_of(b * 512, 512), 512), 256 * k : 256 * k + 256])
            out = part if out is None else out + part
        return out

    def pull_q(b, _):
        acc2[b] = pull(0, b)
        return 0

    lax.fori_loop(0, 4, pull_q, 0)

    from_owners(lambda s: b_in(1, s))
    unpack(1)

    def grad_v(h, _):
        v_rows = pl.ds(pl.multiple_of(64 * h, 64), 64)
        d_rows = pl.ds(pl.multiple_of(64 * lax.rem(h, 2), 64), 64)
        dvt[v_rows, :] += nn(sextt[h // 2, d_rows, :], feat[1, h])
        return 0

    def grad_k(h, _):
        dfe[...] = nn(sext[h // 2, 0:NF, :].astype(BF), vtm[h])
        feature_grad(1, h, dst[1, pl.ds(pl.multiple_of(h * SK, SK), SK), :])
        return 0

    lax.fori_loop(0, 4, grad_v, 0)
    copy_v = hand_over(2, dvt[...])
    lax.fori_loop(0, 4, grad_k, 0)
    copy_k = hand_over(1, through_sketch(1))
    copy_v.wait_recv()
    stores += store(2, ov_hbm, 13)
    copy_k.wait_recv()
    stores += store(1, ok_hbm, 15)

    def block(b):
        return acc2[b] + pull(1, b) + pull(2, b)

    rs = [
        rc(rsend.at[i], rrecv.at[i], rs_s.at[i], rs_r.at[i], head=right if i in (0, 2, 4) else left)
        for i in range(6)
    ]
    out = block(far)
    rsend[0] = out[:, 0:256].astype(BF)
    rs[0].start()
    rsend[1] = out[:, 256:512].astype(BF)
    rs[1].start()
    out = block(right)
    rsend[2] = out[:, 256:512].astype(BF)
    rs[2].start()
    keep_a = out[:, 0:256]
    acc2[right, :, 0:256] = keep_a
    out = block(left)
    rsend[3] = out[:, 0:256].astype(BF)
    rs[3].start()
    rs[0].wait_recv()
    rsend[4] = (acc2[right, :, 0:256] + rrecv[0].astype(F32)).astype(BF)
    rs[4].start()
    acc2[left, :, 256:512] = out[:, 256:512]
    rs[1].wait_recv()
    rsend[5] = (acc2[left, :, 256:512] + rrecv[1].astype(F32)).astype(BF)
    rs[5].start()
    acc2[x] = block(x)

    from_owners(t_in)
    whole = tot.at[c]
    copy_t = rc(whole, whole, ex_s.at[7], ex_r.at[7], seq_2=oc)
    copy_t.start()

    def totals(k):
        for p in range(2):
            tmp[0:NF, :] = tot[k, NF * p : NF * p + NF, :].astype(F32)
            part = nn(jnp.transpose(tmp[...]).astype(BF), fsel[...])
            for hh in range(2):
                h = 4 * k + 2 * p + hh
                dps[h] = dev[h] + part[64 * hh : 64 * hh + 64, :]
        zst[...] = tot[k, ZROW:WIRE, :].astype(F32)
        for j in range(5):
            zpad[pl.ds(pl.multiple_of(8 * k, 8), 4), 128 * j : 128 * j + 128] = zst[4 * j : 4 * j + 4, :]

    def put_state(k, sem):
        heads = pl.ds(4 * k, 4)
        return pltpu.make_async_copy(dps.at[heads], os_hbm.at[heads], loc.at[sem])

    totals(c)
    put_state(c, 17).start()
    copy_t.wait_recv()
    totals(oc)
    put_state(oc, 18).start()
    norms = nn(zpad[0:16, :].astype(BF), fsel[...])
    dpn[0:4, :] = dnv[0:4, :] + norms[0:4, :]
    dpn[4:8, :] = dnv[4:8, :] + norms[8:12, :]
    put_norm = pltpu.make_async_copy(dpn, on_hbm, loc.at[19])
    put_norm.start()

    rs[2].wait_recv()
    rs[3].wait_recv()
    rs[4].wait_recv()
    oin[:, 0:256] = (acc2[x, :, 0:256] + rrecv[3].astype(F32) + rrecv[4].astype(F32)).astype(BF)
    rs[5].wait_recv()
    oin[:, 256:512] = (acc2[x, :, 256:512] + rrecv[2].astype(F32) + rrecv[5].astype(F32)).astype(BF)
    put_in = pltpu.make_async_copy(oin, oi_hbm, loc.at[20])
    put_in.start()

    for one in ag + list(cqkv.values()) + [cga, copy_q, copy_v, copy_k, copy_t] + rs:
        one.wait_send()

    def rest_sent(d, _):
        r = lax.rem(m + d, CH)

        @pl.when(r < OWN)
        def _():
            a_copy(1, r).wait_send()

        @pl.when(m < OWN)
        def _():
            b_copy(0, r).wait_send()
            b_copy(1, r).wait_send()
            t_copy(r).wait_send()

        return 0

    lax.fori_loop(1, CH, rest_sent, 0)
    for one in stores:
        one.wait()
    put_state(c, 17).wait()
    put_state(oc, 18).wait()
    put_norm.wait()
    put_in.wait()


def body(x, wq, wk, wv, sketch, prefix_state, prefix_norm, d_attn, d_state, d_norm):
    any_ = pl.BlockSpec(memory_space=pl.ANY)
    out_shape = (
        jax.ShapeDtypeStruct((TOK, 512), BF),
        jax.ShapeDtypeStruct((TOK, 512), BF),
        jax.ShapeDtypeStruct((TOK, 512), BF),
        jax.ShapeDtypeStruct((TOK, 512), BF),
        jax.ShapeDtypeStruct((8, 64, 1024), F32),
        jax.ShapeDtypeStruct((8, 1024), F32),
    )
    v = pltpu.VMEM
    scratch = [
        v((8, TOK, 256), BF),
        v((3, 2048, 512), BF),
        v((3, TOK, 512), F32),
        v((3, 2, TOK, 256), BF),
        v((3, TOK, 256), BF),
        v((2, TOK, 256), BF),
        v((2, SK, 64), F32),
        v((4, 64, 1024), F32),
        v((8, 1024), F32),
        v((8, 64, 1024), F32),
        v((8, 1024), F32),
        v((8, 64, 1024), F32),
        v((8, 1024), F32),
        v((256, 256), F32),
        v((256, 256), BF),
        v((256, 256), BF),
        v((2, 256, 256), BF),
        v((2, 256, CT), F32),
        v((2, 128, CT), F32),
        v((2, 128, CT), BF),
        v((2, CT, 128), BF),
        v((2, 4, NP, CT), BF),
        v((4, 256, CT), BF),
        v((2, CT, 256), BF),
        v((4, 256, CT), BF),
        v((NP, 384), F32),
        v((384, 1024), BF),
        v((NP, 1024), BF),
        v((4, 144, CT), F32),
        v((256, CT), F32),
        v((4, CT, CT), BF),
        v((4, CT, CT), BF),
        v((4, CT, CT), BF),
        v((144, CT), F32),
        v((NP, 128), F32),
        v((SK, 128), F32),
        v((128, NP), F32),
        v((NF, CT), F32),
        v((2, 128, CT), F32),
        v((256, CT), F32),
        v((2, NP, 256), F32),
        v((2, 144, NP), BF),
        v((WIRE, 128), BF),
        v((2, CH, ROWS, 128), BF),
        v((2, CH, ROWS, 128), BF),
        v((2, WIRE, 128), BF),
        v((ROWS, 128), BF),
        v((2, WIRE, 128), BF),
        v((3, CT, 256), BF),
        v((3, 2, TOK, 256), BF),
        v((4, TOK, 512), F32),
        v((6, TOK, 256), BF),
        v((6, TOK, 256), BF),
        v((TOK, 512), BF),
    ]
    sem = pltpu.SemaphoreType.DMA
    scratch += [
        sem((21,)), sem((6,)), sem((6,)), sem((8,)), sem((8,)), sem((2, CH)), sem((2, CH)),
        sem((2, CH)), sem((2, CH)), sem((CH,)), sem((CH,)), sem((6,)), sem((6,)),
    ]
    swap = (0, 2, 1)
    outs = pl.pallas_call(
        kernel,
        out_shape=out_shape,
        in_specs=[any_] * 10,
        out_specs=(any_,) * 6,
        scratch_shapes=scratch,
        compiler_params=pltpu.CompilerParams(
            collective_id=0, has_side_effects=True, vmem_limit_bytes=60 * 1024 * 1024
        ),
        name="sketch_bwd",
    )(
        x, wq, wk, wv, jnp.transpose(sketch, swap), jnp.transpose(prefix_state, swap),
        prefix_norm, d_attn, jnp.transpose(d_state, swap), d_norm,
    )
    return outs[:4] + (jnp.transpose(outs[4], swap), outs[5])


def solution(mesh):
    finer = Mesh(
        mesh.devices.reshape(4, 4, 2, mesh.shape["head"]), ("seq_0", "seq_1", "seq_2", "head")
    )
    state, rows = P("head", None, None), P("head", None)
    tokens, weight = P(SEQ, "head"), P(None, "head")
    return jax.shard_map(
        body,
        mesh=finer,
        in_specs=(tokens, weight, weight, weight, P(), state, rows, tokens, state, rows),
        out_specs=(tokens, tokens, tokens, tokens, state, rows),
        check_vma=False,
    )
```

time: 526 us -> 80.1 us (0.15)
  waiting for transfers between devices: 212 us -> 0 us
  matrix products: 128 us -> 0 us
  Pallas kernels: 0 us -> 70.5 us
  other arithmetic: 64.2 us -> 0 us
  blocking collectives: 45.9 us -> 0 us
  local copies, waits for them, and re-layouts: 49.9 us -> 8.76 us
  between operations: 14.9 us -> 0.66 us
  starting transfers between devices: 9.05 us -> 0 us
    all_gather x6 -> x0, waiting for transfers between devices: 135 us -> none  [the longest x3 74.4 us: prefix_by_axis(): lax.all_gather(part.astype(kind), axis)]
    dot_general x32 -> x0, matrix products: 128 us -> none  [the longest x3 36 us: attend_block(): jnp.einsum('hif,hfd->hid', feat_query, value_state, precision=HIGHEST_PRE...]
    pallas_call x0 -> x1, Pallas kernels: none -> 70.5 us  [body(): pl.pallas_call(kernel, out_shape=out_shape, in_specs=[any_] * 10, out_spe...]
    psum x1 -> x0, waiting for transfers between devices: 62 us -> none  [packed_total(): subtotal = lax.psum(jnp.concatenate([a.ravel() for a in arrays]), axis)]
    all_gather x6 -> x0, blocking collectives: 45.9 us -> none  [the longest x3 24.2 us: prefix_by_axis(): lax.all_gather(part.astype(kind), axis)]
    reduce_sum x4 -> x0, other arithmetic: 24.4 us -> none  [the longest x3 23.5 us: square_features(): outer_prod = sketched[:, :, :, None] * sketched[:, :, None, :]]
    add x6 -> x0, other arithmetic: 20 us -> none  [the longest x1 5.87 us: body(): state_after = d_state_end + state_after]
    add_any x2 -> x0, local copies, waits for them, and re-layouts: 18.3 us -> none  [the longest x1 9.16 us: attend_block(): jnp.einsum('hif,hfd->hid', feat_query, value_state, precision=HIGHEST_PRE...]
  transfers between devices with their start and end apart: 9 -> 0, of which waited for: 6 -> 0; matrix products, arithmetic and copies ran while one was open for 36% -> 0% of each run, Pallas kernels for 0% -> 0%
where the time goes in v1:
time: 80.1 us; the launch traced here: 79.9 us
  Pallas kernels  70.5 us (88%)
  local copies, waits for them, and re-layouts  8.76 us (11%)
    pallas_call x1, Pallas kernels, body(): pl.pallas_call(kernel, out_shape=out_shape, in_specs=[any_] * 10, out_spe...  70.5 us
    unnamed x10, local copies, waits for them, and re-layouts  8.76 us

profile of v1, /device:TPU:1, one launch (start us, length us, event | category | flops | bytes accessed | tf_op | source)
XLA Modules:
  0.0 79.9 jit_solution(778494517507593405)
XLA Ops:
  0.6 70.5 %sketch_bwd.1 = (bf16[256,512]{1,0:T(8,128)(2,1)}, bf16[256,512]{1,0:T(8,128)(2,1)}, bf16[256,512]{1,0:T(8,128)(2,1)}, bf16[256,512]{1,0:T(8,128)(2,1)}, f32[8,64,1024]{2,1,0:T(8,128)}, /*index=5*/f32[8,1024]{1,0:T(8,128)}) custom-call(bf16[256,512]{1,0:T(8,128)(2,1)} %x_hbm.1, bf16[2048,512]{1,0:T(8,128)(2,1)} %wq_hbm.1, bf16[2048,512]{1,0:T(8,128)(2,1)} %wk_hbm.1, ...), custom_call_target="tpu_custom_call" | custom-call | tf_op jit(solution)/shard_map/sketch_bwd/pallas_call | solution.py:716
  71.1 0.0 copy-start
  71.1 1.8 %copy.22 = bf16[256,512]{1,0:T(8,128)(2,1)} copy(bf16[256,512]{1,0:T(8,128)(2,1)} %get-tuple-element.24) | data formatting | bytes 524288
  72.9 1.7 %copy.23 = bf16[256,512]{1,0:T(8,128)(2,1)} copy(bf16[256,512]{1,0:T(8,128)(2,1)} %get-tuple-element.25) | data formatting | bytes 524288
  74.6 1.7 %copy.24 = bf16[256,512]{1,0:T(8,128)(2,1)} copy(bf16[256,512]{1,0:T(8,128)(2,1)} %get-tuple-element.26) | data formatting | bytes 524288
  76.3 1.7 %copy.25 = bf16[256,512]{1,0:T(8,128)(2,1)} copy(bf16[256,512]{1,0:T(8,128)(2,1)} %get-tuple-element.27) | data formatting | bytes 524288
  77.9 0.0 copy-done
  77.9 0.0 copy-start.1
  77.9 1.3 %copy.26 = f32[8,1024,64]{1,2,0:T(8,128)} copy(f32[8,1024,64]{1,2,0:T(8,128)S(1)} %bitcast.4) | data formatting | bytes 4194304
  79.3 0.0 copy-done.1
  79.3 0.6 copy.27
Async XLA Ops:
  71.1 6.8 %copy-start = (f32[8,64,1024]{2,1,0:T(8,128)S(1)}, f32[8,64,1024]{2,1,0:T(8,128)}, u32[]{:S(2)}) copy-start(f32[8,64,1024]{2,1,0:T(8,128)} %get-tuple-element.16) | copy-start | bytes 6291460
  77.9 1.3 %copy-start.1 = (f32[8,1024]{1,0:T(8,128)S(1)}, f32[8,1024]{1,0:T(8,128)}, u32[]{:S(2)}) copy-start(f32[8,1024]{1,0:T(8,128)} %get-tuple-element.29) | copy-start | bytes 98308

commit v2 on v1

v2 whole, which is shorter than its diff:
```python
import jax
import jax.numpy as jnp
from jax import lax
from jax.experimental import pallas as pl
from jax.experimental.pallas import tpu as pltpu
from jax.sharding import Mesh
from jax.sharding import PartitionSpec as P

SEQ = ("seq_0", "seq_1", "seq_2")
MESH = pl.DeviceIdType.MESH
F32 = jnp.float32
BF = jnp.bfloat16

SK = 32
NS = 17
NF = NS * SK
NP = 640
TOK = 256
CT = 512
CH = 16
ROWS = 80
OWN = 14
WIRE = OWN * ROWS
FAR_FIRST = (10, 9, 11, 6, 14, 2, 8, 5, 7, 13, 15, 1, 3, 4, 12)
ZROW = 2 * NF
SPLIT = NF // ROWS


def nn(a, b):
    return lax.dot_general(a, b, (((1,), (0,)), ((), ())), preferred_element_type=F32)


def nt(a, b):
    return lax.dot_general(a, b, (((1,), (1,)), ((), ())), preferred_element_type=F32)


def kernel(
    x_hbm, wq_hbm, wk_hbm, wv_hbm, g_hbm, ps_hbm, pn_hbm, da_hbm, de_hbm, dn_hbm,
    oin, oqkv, dps, dpn,
    xg, w, acc, qkv, xsend, ga, gt, psv, pnv, dev, dnv,
    bd, bdh, bdl, bdt, lrt, skt, skb, stok, feat, vtm, vtok, dext, fold, stk, fsel,
    yloc, gtr, scr, dmat, wmat, yv, tmp, zst, zpad, dfe, dst, dvt, sext, sextt, sextb,
    wire, inb, outb, res, totb, tot, dtok, dall, acc2, rsend, rrecv,
    loc, ag_s, ag_r, ex_s, ex_r, a_s, a_r, b_s, b_r, t_s, t_r, rs_s, rs_r,
):
    y = lax.axis_index("seq_0")
    z = lax.axis_index("seq_1")
    c = lax.axis_index("seq_2")
    x = lax.axis_index("head")
    m = y * 4 + z
    oc = 1 - c
    right, left, far = lax.rem(x + 1, 4), lax.rem(x + 3, 4), lax.rem(x + 2, 4)

    def rc(src, dst_, ss, rs, **where):
        return pltpu.make_async_remote_copy(
            src_ref=src, dst_ref=dst_, send_sem=ss, recv_sem=rs,
            device_id=where, device_id_type=MESH,
        )

    own_cols = pl.ds(pl.multiple_of(c * 256, 256), 256)
    oth_cols = pl.ds(pl.multiple_of(oc * 256, 256), 256)

    lx = [
        pltpu.make_async_copy(x_hbm.at[:, 256 * k : 256 * k + 256], xg.at[2 * x + k], loc.at[k])
        for k in range(2)
    ]
    lw = [
        pltpu.make_async_copy(src, w.at[t], loc.at[2 + t])
        for t, src in enumerate((wq_hbm, wk_hbm, wv_hbm))
    ]
    lg = pltpu.make_async_copy(g_hbm, gt, loc.at[5])
    la = pltpu.make_async_copy(da_hbm.at[:, own_cols], ga.at[c], loc.at[6])
    ln = pltpu.make_async_copy(pn_hbm, pnv, loc.at[7])
    lp = pltpu.make_async_copy(ps_hbm.at[pl.ds(4 * c, 4)], psv, loc.at[8])
    le = pltpu.make_async_copy(de_hbm, dev, loc.at[9])
    lm = pltpu.make_async_copy(dn_hbm, dnv, loc.at[10])
    for copy in (lx[0], lx[1], lw[1], lw[2], lw[0], lg, la, ln, lp, le, lm):
        copy.start()

    bar = pltpu.get_barrier_semaphore()
    for peer in (right, left):
        pl.semaphore_signal(bar, inc=1, device_id={"head": peer}, device_id_type=MESH)
    pl.semaphore_signal(bar, inc=1, device_id={"seq_2": oc}, device_id_type=MESH)

    def greet(d, _):
        r = lax.rem(m + d, CH)
        pl.semaphore_signal(
            bar, inc=1, device_id={"seq_0": r // 4, "seq_1": lax.rem(r, 4)}, device_id_type=MESH
        )
        return 0

    lax.fori_loop(1, CH, greet, 0)
    pl.semaphore_wait(bar, 18)

    def slab(src, k, peer, i):
        ref = xg.at[2 * src + k]
        return rc(ref, ref, ag_s, ag_r.at[i], head=peer)

    ag = [
        slab(x, 0, right, 0), slab(x, 1, left, 1), slab(x, 1, right, 2), slab(x, 0, left, 3),
        slab(left, 0, right, 4), slab(right, 1, left, 5),
    ]
    lx[0].wait()
    lx[1].wait()
    for i in range(4):
        ag[i].start()
    cga = rc(da_hbm.at[:, oth_cols], ga.at[c], ex_s.at[0], ex_r.at[0], seq_2=oc)
    cga.start()

    lg.wait()
    bd[...] = jnp.zeros((256, 256), F32)
    lane128 = lax.broadcasted_iota(jnp.int32, (SK, 128), 1) // 64
    for lr in range(2):
        wide = jnp.concatenate([gt[lr], gt[lr]], axis=1)
        for h in range(4):
            row = lr * 128 + h * SK
            col = 128 * (h // 2)
            bd[row : row + SK, col : col + 128] = jnp.where(lane128 == h % 2, wide, 0.0)
    bdh[...] = bd[...].astype(BF)
    bdl[...] = (bd[...] - bdh[...].astype(F32)).astype(BF)
    bdt[0] = jnp.transpose(bd[...]).astype(BF)
    bdt[1] = (jnp.transpose(bd[...]) - bdt[0].astype(F32)).astype(BF)

    for t in range(3):
        lw[(1, 2, 0)[t]].wait()

    def project(src, first):
        for t in range(3):
            out = nn(xg[2 * src], w[t, pl.ds(pl.multiple_of(src * 512, 512), 256), :])
            out = out + nn(xg[2 * src + 1], w[t, pl.ds(pl.multiple_of(src * 512 + 256, 256), 256), :])
            if first:
                acc[t] = out
            else:
                acc[t] += out

    project(x, True)
    ag[0].wait_recv()
    ag[4].start()
    ag[1].wait_recv()
    ag[5].start()

    def build(i, _):
        f = lax.broadcasted_iota(jnp.int32, (SK, 1024), 1)
        fi, fj = f // SK, lax.rem(f, SK)
        a = lax.broadcasted_iota(jnp.int32, (SK, 1024), 0)
        b = lax.rem(a + i, SK)
        hit = ((fi == a) & (fj == b)) | ((fi == b) & (fj == a))
        value = jnp.where(i == 16, 0.5, 1.0)
        keep = jnp.where(i < NS, value, 0.0)
        fsel[pl.ds(pl.multiple_of(i * SK, SK), SK), :] = jnp.where(hit, keep, 0.0).astype(BF)
        return 0

    lax.fori_loop(0, NP // SK, build, 0)
    for h in range(4):
        for q in range(2):
            feat[q, h, NF:NP, :] = jnp.zeros((NP - NF, CT), BF)
    zpad[...] = jnp.zeros((128, NP), F32)
    tmp[...] = jnp.zeros((NP, 128), F32)
    dext[...] = jnp.zeros(dext.shape, BF)
    stk[...] = jnp.zeros(stk.shape, BF)
    zst[...] = jnp.zeros((SK, 128), F32)
    vtm[...] = jnp.zeros(vtm.shape, BF)
    sext[...] = jnp.zeros(sext.shape, F32)

    ag[2].wait_recv()
    project(left, False)
    ag[3].wait_recv()
    project(right, False)
    ag[4].wait_recv()
    ag[5].wait_recv()

    cqkv = {}

    def last_projection(t):
        cqkv[t] = rc(xsend.at[t], qkv.at[t, c], ex_s.at[1 + t], ex_r.at[1 + t], seq_2=oc)
        for cols, target in ((oth_cols, None), (own_cols, c)):
            out = acc[t, :, cols] + nn(
                xg[2 * far], w[t, pl.ds(pl.multiple_of(far * 512, 512), 256), cols]
            )
            out = out + nn(
                xg[2 * far + 1], w[t, pl.ds(pl.multiple_of(far * 512 + 256, 256), 256), cols]
            )
            if target is None:
                xsend[t] = out.astype(BF)
                cqkv[t].start()
            else:
                qkv[t, target] = out.astype(BF)

    last_projection(1)
    last_projection(2)

    scale = SK ** (-0.5)

    def eights(v, k):
        return v if k == 0 else jnp.concatenate([v[8 * k :], v[: 8 * k]], axis=0)

    def ones(v, k):
        return v if k == 0 else pltpu.roll(v, SK - k, 0)

    def sketch(t, k):
        part = pl.ds(pl.multiple_of(256 * k, 256), 256)
        src = qkv[t, k]
        lr = nt(bdh[...], src) + nt(bdl[...], src)
        lrt[t, :, part] = lr
        tok = nt(src, bdh[...]) + nt(src, bdl[...])
        stok[t, part, :] = (tok[:, :128] * tok[:, 128:] * scale).astype(BF)
        st = lr[:128] * lr[128:] * scale
        skt[t, :, part] = st
        skb[t, :, part] = st.astype(BF)

        def one(h, _):
            for q in range(2):
                cols = pl.ds(pl.multiple_of(256 * k + 128 * q, 128), 128)
                s = skt[t, pl.ds(pl.multiple_of(h * SK, SK), SK), cols]
                for b in range(8):
                    turned = ones(s, b)
                    for a in range(3 if b == 0 else 2):
                        i = 8 * a + b
                        feat[t, h, SK * i : SK * i + SK, cols] = (s * eights(turned, a)).astype(BF)
            return 0

        lax.fori_loop(0, 4, one, 0)

    lane256 = lax.broadcasted_iota(jnp.int32, (CT, 256), 1)

    def pack_z(n, total):
        tmp[0:NF, :] = total
        zt = jnp.transpose(tmp[...])
        for j in range(5):
            zst[4 * j : 4 * j + 4, :] = zt[0:4, 128 * j : 128 * j + 128]
        wire[n, ZROW:WIRE, :] = zst[...].astype(BF)

    def others():
        for d in FAR_FIRST:
            py, pz = lax.rem(y + d // 4, 4), lax.rem(z + d % 4, 4)
            yield py * 4 + pz, {"seq_0": py, "seq_1": pz}

    def scan_send(n, lo, hi):
        for r, where in others():

            @pl.when((r >= lo) & (r < hi))
            def _(r=r, where=where):
                rc(
                    wire.at[n, pl.ds(pl.multiple_of(r * ROWS, ROWS), ROWS)], inb.at[n, m],
                    a_s.at[n], a_r.at[n], **where,
                ).start()

        @pl.when((m >= lo) & (m < hi))
        def _():
            inb[n, m] = wire[n, pl.ds(pl.multiple_of(m * ROWS, ROWS), ROWS), :]

    def mine(ref):
        return ref.at[pl.ds(pl.multiple_of(m * ROWS, ROWS), ROWS)]

    def scan_own(n, reverse):
        @pl.when(m < OWN)
        def _():
            part = inb.at[n, 0 : CH - 1]
            rc(part, part, t_s, a_r.at[n], seq_2=oc).wait_recv()
            running = jnp.zeros((ROWS, 128), F32)
            for i in range(CH):
                r = CH - 1 - i if reverse else i
                outb[n, r] = running.astype(BF)
                running = running + inb[n, r].astype(F32)
            if reverse:
                totb[...] = running.astype(BF)
            for r, where in others():
                rc(outb.at[n, r], mine(res.at[n]), b_s.at[n], b_r.at[n], **where).start()
            res[n, pl.ds(pl.multiple_of(m * ROWS, ROWS), ROWS), :] = outb[n, m]
            if reverse:
                tot[c, pl.ds(pl.multiple_of(m * ROWS, ROWS), ROWS), :] = totb[...]
                for r, where in others():
                    rc(totb, mine(tot.at[c]), t_s, t_r, **where).start()

    def from_owners(ref, sem):
        def all_of(count):
            part = ref.at[pl.ds(0, count * ROWS)]
            rc(part, part, t_s, sem, seq_2=oc).wait_recv()

        @pl.when(m < OWN)
        def _():
            all_of(OWN - 1)

        @pl.when(m >= OWN)
        def _():
            all_of(OWN)

    def sends_done():
        for n in range(2):
            def all_of(count):
                part = wire.at[n, pl.ds(0, count * ROWS)]
                rc(part, part, a_s.at[n], t_r, seq_2=oc).wait_send()

            @pl.when(m < OWN)
            def _():
                all_of(OWN - 1)
                part = outb.at[n, 0 : CH - 1]
                rc(part, part, b_s.at[n], t_r, seq_2=oc).wait_send()

            @pl.when(m >= OWN)
            def _():
                all_of(OWN)

        @pl.when(m < OWN)
        def _():
            part = outb.at[0, 0 : CH - 1]
            rc(part, part, t_s, t_r, seq_2=oc).wait_send()

    def fold_in(state, norm):
        stk[0:256, :] = state
        pick = jnp.where(c == 0, norm[0:4, :], norm[4:8, :])
        stk[256:272, :] = jnp.concatenate([pick, jnp.zeros((12, 1024), F32)], axis=0).astype(BF)
        fold[...] = nt(fsel[...], stk[...])

    row_w = lax.broadcasted_iota(jnp.int32, (NF, 128), 0)
    weight = jnp.where((row_w < SK) | (row_w >= 16 * SK), 1.0, 2.0)

    def unpack(n):
        zst[...] = res[n, ZROW:WIRE, :].astype(F32)
        for j in range(5):
            zpad[0:4, 128 * j : 128 * j + 128] = zst[4 * j : 4 * j + 4, :]
        zc = jnp.transpose(zpad[...])[0:NF, :] * weight + fold[0:NF, 256:384]
        for p in range(2):
            part = res[n, NF * p : NF * p + NF, :].astype(F32)
            sext[p, 0:NF, 0:128] = part * weight + fold[0:NF, 128 * p : 128 * p + 128]
            sext[p, 0:NF, 128:256] = zc
            sextt[p] = jnp.transpose(sext[p])[0:144, :].astype(BF)

    sketch(1, c)
    cqkv[1].wait_recv()
    sketch(1, oc)
    cqkv[2].wait_recv()
    for p in range(2):
        for k in range(2):
            vtok[p, 256 * k : 256 * k + 256, 0:128] = qkv[2, k, :, 128 * p : 128 * p + 128]
        vtok[p, :, 128:256] = jnp.ones((CT, 128), BF)
    ztot = None
    for p in range(2):
        out = None
        for hh in range(2):
            h = 2 * p + hh
            keep = (lane256 // 64 == hh) | (lane256 == 128 + h)
            vm = jnp.where(keep, vtok[p].astype(F32), 0.0).astype(BF)
            part = nn(feat[1, h, 0:NF, :], vm)
            out = part if out is None else out + part
        wire[0, NF * p : NF * p + NF, :] = out[:, 0:128].astype(BF)
        ztot = out[:, 128:256] if ztot is None else ztot + out[:, 128:256]
        if p == 0:
            scan_send(0, 0, SPLIT)
    pack_z(0, ztot)
    scan_send(0, SPLIT, OWN)


    last_projection(0)
    lp.wait()
    ln.wait()
    fold_in(psv[...].reshape(256, 1024).astype(BF), pnv)
    sketch(0, c)
    cqkv[0].wait_recv()
    sketch(0, oc)

    scan_own(0, False)

    la.wait()
    cga.wait_recv()
    for k in range(2):
        part = slice(256 * k, 256 * k + 256)
        gtr[:, part] = jnp.transpose(ga[k].astype(F32))
        vt = jnp.transpose(qkv[2, k].astype(F32)).astype(BF)
        for h in range(4):
            vtm[h, 64 * (h % 2) : 64 * (h % 2) + 64, part] = vt[64 * h : 64 * h + 64, :]
    row16 = lax.broadcasted_iota(jnp.int32, (16, CT), 0)
    for h in range(4):
        vtm[h, 128:144, :] = jnp.where(row16 == h, 1.0, 0.0).astype(BF)

    diag = lax.broadcasted_iota(jnp.int32, (256, 256), 0) <= lax.broadcasted_iota(
        jnp.int32, (256, 256), 1
    )
    lane_k = lax.broadcasted_iota(jnp.int32, (256, 128), 1) // SK

    def scores(h, _):
        for jb in range(2):
            keys = jnp.where(lane_k == h, stok[1, 256 * jb : 256 * jb + 256, :].astype(F32), 0.0)
            keys = keys.astype(BF)
            for ib in range(jb, 2):
                d = nn(keys, skb[0, :, 256 * ib : 256 * ib + 256])
                if ib == jb:
                    d = jnp.where(diag, d, 0.0)
                at = (h, slice(256 * jb, 256 * jb + 256), slice(256 * ib, 256 * ib + 256))
                scr[at] = (d * d).astype(BF)
                dmat[at] = (d + d).astype(BF)
        yloc[h, :, 0:256] = nn(vtm[h, 0:144, 0:256], scr[h, 0:256, 0:256])
        yloc[h, :, 256:512] = nn(vtm[h, 0:144, :], scr[h, :, 256:512])
        return 0

    lax.fori_loop(0, 4, scores, 0)

    from_owners(res.at[0], b_r.at[0])
    unpack(0)
    ztot = None
    for p in range(2):
        out = None
        for hh in range(2):
            h = 2 * p + hh
            yv[h] = nn(sextt[p], feat[0, h]) + yloc[h]
            num = yv[h, 64 * hh : 64 * hh + 64, :]
            inv = 1.0 / (1.0 + yv[h, 128 + h : 129 + h, :])
            g = gtr[64 * h : 64 * h + 64, :]
            dden = -jnp.sum(g * num, axis=0, keepdims=True) * inv * inv
            dext[h, 64 * hh : 64 * hh + 64, :] = (g * inv).astype(BF)
            dext[h, 128:144, :] = jnp.where(row16 == h, dden, 0.0).astype(BF)
            part = nt(feat[0, h, 0:NF, :], dext[h])
            out = part if out is None else out + part
        wire[1, NF * p : NF * p + NF, :] = out[:, 0:128].astype(BF)
        ztot = out[:, 128:256] if ztot is None else ztot + out[:, 128:256]
        if p == 0:
            scan_send(1, 0, SPLIT)
    pack_z(1, ztot)
    scan_send(1, SPLIT, OWN)

    def lanes(ref, at, u):
        return jnp.concatenate(
            [ref[at + (slice(128 * u, 128 * u + 128),)], ref[at + (slice(256 + 128 * u, 384 + 128 * u),)]],
            axis=1,
        )

    def feature_grad(t, h, u, slot):
        rows = pl.ds(pl.multiple_of(h * SK, SK), SK)
        for q in range(2):
            cols = slice(256 * q + 128 * u, 256 * q + 128 * u + 128)
            mine_ = slice(128 * q, 128 * q + 128)
            s = skt[t, rows, cols]
            here = dst[t, rows, cols] + 2.0 * s * dfe[slot, 0:SK, mine_]
            for b in range(8):
                turned = ones(s, b)
                back = None
                for a in range(3 if b == 0 else 2):
                    i = 8 * a + b
                    if i == 0:
                        continue
                    d = dfe[slot, SK * i : SK * i + SK, mine_]
                    here = here + d * eights(turned, a)
                    term = eights(d * s, (4 - a) % 4)
                    back = term if back is None else back + term
                here = here + (back if b == 0 else pltpu.roll(back, b, 0))
            dst[t, rows, cols] = here

    def local_grads(h, _):
        p = h // 2
        for jb in range(2):
            for ib in range(jb, 2):
                at = (h, slice(256 * jb, 256 * jb + 256), slice(256 * ib, 256 * ib + 256))
                ds = nn(vtok[p, 256 * jb : 256 * jb + 256, :], dext[h, :, 256 * ib : 256 * ib + 256])
                wmat[at] = (dmat[at].astype(F32) * ds).astype(BF)
        sk_rows = pl.ds(pl.multiple_of(h * SK, SK), SK)
        d_rows = pl.ds(pl.multiple_of(64 * lax.rem(h, 2), 64), 64)
        v_rows = pl.ds(pl.multiple_of(64 * h, 64), 64)
        dst[0, sk_rows, 0:256] = nn(skb[1, sk_rows, 0:256], wmat[h, 0:256, 0:256])
        dst[0, sk_rows, 256:512] = nn(skb[1, sk_rows, :], wmat[h, :, 256:512])
        dst[1, sk_rows, 0:256] = nt(skb[0, sk_rows, :], wmat[h, 0:256, :])
        dst[1, sk_rows, 256:512] = nt(skb[0, sk_rows, 256:512], wmat[h, 256:512, 256:512])
        dvt[v_rows, 0:256] = nt(dext[h, d_rows, :], scr[h, 0:256, :])
        dvt[v_rows, 256:512] = nt(dext[h, d_rows, 256:512], scr[h, 256:512, 256:512])
        return 0

    def through_sketch(t, u):
        at = (slice(0, 128),)
        lt, rt = lanes(lrt.at[t], at, u), lanes(lrt.at[t], (slice(128, 256),), u)
        ds = lanes(dst.at[t], at, u) * scale
        dlr = jnp.concatenate([ds * rt, ds * lt], axis=0).astype(BF)
        return nn(bdt[0], dlr) + nn(bdt[1], dlr)

    def keep(t, u, grad):
        dtok[u, t] = jnp.transpose(grad).astype(BF)
        dall[t, c, 128 * u : 128 * u + 128, :] = dtok[
            u, t, pl.ds(pl.multiple_of(128 * c, 128), 128), :
        ]

    oth_half = pl.ds(pl.multiple_of(128 * oc, 128), 128)

    def hand_q(u):
        copy = rc(
            dtok.at[u, 0, oth_half], dall.at[0, c, 128 * u : 128 * u + 128],
            ex_s.at[4 + u], ex_r.at[4 + u], seq_2=oc,
        )
        copy.start()
        return copy

    def hand_kv(u):
        copy = rc(
            dtok.at[u, 1:3, oth_half], dall.at[1:3, c, 128 * u : 128 * u + 128],
            ex_s.at[6 + u], ex_r.at[6 + u], seq_2=oc,
        )
        copy.start()
        return copy

    lax.fori_loop(0, 4, local_grads, 0)

    copy_q = []
    for u in range(2):

        def grad_q(p, _, u=u):
            for hh in range(2):
                h = 2 * p + hh
                dfe[hh] = nn(sext[p, 0:NF, :].astype(BF), lanes(dext.at[h], (slice(0, 256),), u))
                feature_grad(0, h, u, hh)
            return 0

        lax.fori_loop(0, 2, grad_q, 0)
        keep(0, u, through_sketch(0, u))
        copy_q.append(hand_q(u))
    scan_own(1, True)

    le.wait()
    lm.wait()
    fold_in(dev[pl.ds(4 * c, 4)].reshape(256, 1024).astype(BF), dnv)
    for u in range(2):
        copy_q[u].wait_recv()

    def pull(t, b, rows):
        out = None
        for k in range(2):
            part = nt(
                dall[t, k, rows], w[t, pl.ds(pl.multiple_of(b * 512, 512), 512), 256 * k : 256 * k + 256]
            )
            out = part if out is None else out + part
        return out

    def pull_q(b, _):
        acc2[b] = pull(0, b, slice(0, 256))
        return 0

    lax.fori_loop(0, 4, pull_q, 0)

    from_owners(res.at[1], b_r.at[1])
    unpack(1)

    def grads(u):
        for h in range(4):
            v_rows = slice(64 * h, 64 * h + 64)
            d_rows = slice(64 * (h % 2), 64 * (h % 2) + 64)
            out = nn(sextt[h // 2, d_rows, :], lanes(feat.at[1, h], (slice(0, NP),), u))
            for q in range(2):
                cols = slice(256 * q + 128 * u, 256 * q + 128 * u + 128)
                dvt[v_rows, cols] += out[:, 128 * q : 128 * q + 128]
        keep(2, u, lanes(dvt, (slice(0, 256),), u))
        for h in range(4):
            dfe[h] = nn(sextb[h // 2], lanes(vtm.at[h], (slice(0, 256),), u))
            feature_grad(1, h, u, h)
        keep(1, u, through_sketch(1, u))
        return hand_kv(u)

    for p in range(2):
        sextb[p] = sext[p, 0:NF, :].astype(BF)
    copy_kv = [grads(0)]
    copy_kv.append(grads(1))

    rs = [
        [
            rc(
                rsend.at[u, i], rrecv.at[u, i], rs_s, rs_r.at[u, i],
                head=right if i in (0, 2, 4) else left,
            )
            for i in range(6)
        ]
        for u in range(2)
    ]

    def block(b, u):
        rows = slice(128 * u, 128 * u + 128)
        return acc2[b, rows, :] + pull(1, b, rows) + pull(2, b, rows)

    def outgoing(u):
        rows = slice(128 * u, 128 * u + 128)
        out = block(far, u)
        rsend[u, 0] = out[:, 0:256].astype(BF)
        rs[u][0].start()
        rsend[u, 1] = out[:, 256:512].astype(BF)
        rs[u][1].start()
        out = block(right, u)
        rsend[u, 2] = out[:, 256:512].astype(BF)
        rs[u][2].start()
        acc2[right, rows, 0:256] = out[:, 0:256]
        out = block(left, u)
        rsend[u, 3] = out[:, 0:256].astype(BF)
        rs[u][3].start()
        acc2[left, rows, 256:512] = out[:, 256:512]

    def merge(u):
        rows = slice(128 * u, 128 * u + 128)
        rs[u][0].wait_recv()
        rsend[u, 4] = (acc2[right, rows, 0:256] + rrecv[u, 0].astype(F32)).astype(BF)
        rs[u][4].start()
        rs[u][1].wait_recv()
        rsend[u, 5] = (acc2[left, rows, 256:512] + rrecv[u, 1].astype(F32)).astype(BF)
        rs[u][5].start()

    def arrived(u):
        rows = slice(128 * u, 128 * u + 128)
        rs[u][3].wait_recv()
        rs[u][4].wait_recv()
        oin[rows, 0:256] = (
            acc2[x, rows, 0:256] + rrecv[u, 3].astype(F32) + rrecv[u, 4].astype(F32)
        ).astype(BF)
        rs[u][2].wait_recv()
        rs[u][5].wait_recv()
        oin[rows, 256:512] = (
            acc2[x, rows, 256:512] + rrecv[u, 2].astype(F32) + rrecv[u, 5].astype(F32)
        ).astype(BF)

    copy_kv[0].wait_recv()
    outgoing(0)
    copy_kv[1].wait_recv()
    outgoing(1)
    merge(0)
    for u in range(2):
        acc2[x, 128 * u : 128 * u + 128, :] = block(x, u)
    merge(1)
    for t in range(3):
        for k in range(2):
            oqkv[t, :, 256 * k : 256 * k + 256] = dall[t, k]

    from_owners(tot.at[c], t_r)
    whole = tot.at[c]
    copy_t = rc(whole, whole, ex_s.at[8], ex_r.at[8], seq_2=oc)
    copy_t.start()

    def totals(k):
        for p in range(2):
            tmp[0:NF, :] = tot[k, NF * p : NF * p + NF, :].astype(F32)
            part = nn(jnp.transpose(tmp[...]).astype(BF), fsel[...])
            for hh in range(2):
                h = 4 * k + 2 * p + hh
                dps[h] = dev[h] + part[64 * hh : 64 * hh + 64, :]
        zst[...] = tot[k, ZROW:WIRE, :].astype(F32)
        for j in range(5):
            zpad[pl.ds(pl.multiple_of(8 * k, 8), 4), 128 * j : 128 * j + 128] = zst[4 * j : 4 * j + 4, :]

    totals(c)
    copy_t.wait_recv()
    totals(oc)
    norms = nn(zpad[0:16, :].astype(BF), fsel[...])
    dpn[0:4, :] = dnv[0:4, :] + norms[0:4, :]
    dpn[4:8, :] = dnv[4:8, :] + norms[8:12, :]

    arrived(0)
    arrived(1)

    sends = xg.at[0:6]
    rc(sends, sends, ag_s, t_r, seq_2=oc).wait_send()
    for one in list(cqkv.values()) + [cga, copy_t] + copy_q + copy_kv:
        one.wait_send()
    sends = rsend.at[:]
    rc(sends, sends, rs_s, t_r, seq_2=oc).wait_send()
    sends_done()


def put_kernel(oin, oqkv, dps, dpn, oi_hbm, oq_hbm, ok_hbm, ov_hbm, os_hbm, on_hbm, sem):
    copies = [
        pltpu.make_async_copy(dps.at[4 * k : 4 * k + 4], os_hbm.at[4 * k : 4 * k + 4], sem.at[k])
        for k in range(2)
    ]
    copies += [
        pltpu.make_async_copy(oqkv.at[t], ref, sem.at[2 + t])
        for t, ref in enumerate((oq_hbm, ok_hbm, ov_hbm))
    ]
    copies.append(pltpu.make_async_copy(oin, oi_hbm, sem.at[5]))
    copies.append(pltpu.make_async_copy(dpn, on_hbm, sem.at[6]))
    for copy in copies:
        copy.start()
    for copy in copies:
        copy.wait()


def body(x, wq, wk, wv, sketch, prefix_state, prefix_norm, d_attn, d_state, d_norm):
    any_ = pl.BlockSpec(memory_space=pl.ANY)
    v = pltpu.VMEM
    scratch = [
        v((8, TOK, 256), BF),
        v((3, 2048, 512), BF),
        v((3, TOK, 512), F32),
        v((3, 2, TOK, 256), BF),
        v((3, TOK, 256), BF),
        v((2, TOK, 256), BF),
        v((2, SK, 64), F32),
        v((4, 64, 1024), F32),
        v((8, 1024), F32),
        v((8, 64, 1024), F32),
        v((8, 1024), F32),
        v((256, 256), F32),
        v((256, 256), BF),
        v((256, 256), BF),
        v((2, 256, 256), BF),
        v((2, 256, CT), F32),
        v((2, 128, CT), F32),
        v((2, 128, CT), BF),
        v((2, CT, 128), BF),
        v((2, 4, NP, CT), BF),
        v((4, 256, CT), BF),
        v((2, CT, 256), BF),
        v((4, 256, CT), BF),
        v((NP, 384), F32),
        v((384, 1024), BF),
        v((NP, 1024), BF),
        v((4, 144, CT), F32),
        v((256, CT), F32),
        v((4, CT, CT), BF),
        v((4, CT, CT), BF),
        v((4, CT, CT), BF),
        v((4, 144, CT), F32),
        v((NP, 128), F32),
        v((SK, 128), F32),
        v((128, NP), F32),
        v((4, NF, 256), F32),
        v((2, 128, CT), F32),
        v((256, CT), F32),
        v((2, NP, 256), F32),
        v((2, 144, NP), BF),
        v((2, NF, 256), BF),
        v((2, WIRE, 128), BF),
        v((2, CH, ROWS, 128), BF),
        v((2, CH, ROWS, 128), BF),
        v((2, WIRE, 128), BF),
        v((ROWS, 128), BF),
        v((2, WIRE, 128), BF),
        v((2, 3, 256, 256), BF),
        v((3, 2, TOK, 256), BF),
        v((4, TOK, 512), F32),
        v((2, 6, 128, 256), BF),
        v((2, 6, 128, 256), BF),
    ]
    sem = pltpu.SemaphoreType.DMA
    scratch += [
        sem((11,)), sem, sem((6,)), sem((9,)), sem((9,)), sem((2,)), sem((2,)),
        sem((2,)), sem((2,)), sem, sem, sem, sem((2, 6)),
    ]
    swap = (0, 2, 1)
    made = (
        v((TOK, 512), BF),
        v((3, TOK, 512), BF),
        v((8, 64, 1024), F32),
        v((8, 1024), F32),
    )
    held = pl.BlockSpec(memory_space=pltpu.VMEM)
    outs = pl.pallas_call(
        kernel,
        out_shape=made,
        in_specs=[any_] * 10,
        out_specs=(held,) * 4,
        scratch_shapes=scratch,
        compiler_params=pltpu.CompilerParams(
            collective_id=0, has_side_effects=True, vmem_limit_bytes=60 * 1024 * 1024
        ),
        name="sketch_bwd",
    )(
        x, wq, wk, wv, jnp.transpose(sketch, swap), jnp.transpose(prefix_state, swap),
        prefix_norm, d_attn, jnp.transpose(d_state, swap), d_norm,
    )
    rows = jax.ShapeDtypeStruct((TOK, 512), BF)
    outs = pl.pallas_call(
        put_kernel,
        out_shape=(
            rows, rows, rows, rows,
            jax.ShapeDtypeStruct((8, 64, 1024), F32),
            jax.ShapeDtypeStruct((8, 1024), F32),
        ),
        in_specs=[held] * 4,
        out_specs=(any_,) * 6,
        scratch_shapes=[sem((7,))],
        compiler_params=pltpu.CompilerParams(vmem_limit_bytes=1024 * 1024),
        name="put_out",
    )(*(pltpu.with_memory_space_constraint(o, pltpu.VMEM) for o in outs))
    return outs[:4] + (jnp.transpose(outs[4], swap), outs[5])


def solution(mesh):
    finer = Mesh(
        mesh.devices.reshape(4, 4, 2, mesh.shape["head"]), ("seq_0", "seq_1", "seq_2", "head")
    )
    state, rows = P("head", None, None), P("head", None)
    tokens, weight = P(SEQ, "head"), P(None, "head")
    return jax.shard_map(
        body,
        mesh=finer,
        in_specs=(tokens, weight, weight, weight, P(), state, rows, tokens, state, rows),
        out_specs=(tokens, tokens, tokens, tokens, state, rows),
        check_vma=False,
    )
```

time: 80.1 us -> 66.2 us (0.83)
  local copies, waits for them, and re-layouts: 8.76 us -> 0 us
  Pallas kernels: 70.5 us -> 65.3 us
    unnamed x10 -> x0, local copies, waits for them, and re-layouts: 8.76 us -> none
    pallas_call x1 -> x2, Pallas kernels: 70.5 us -> 65.3 us  [the longest x1 63.6 us: body(): pl.pallas_call(kernel, out_shape=made, in_specs=[any_] * 10, out_specs=(h...]
where the time goes in v2:
time: 66.2 us; the launch traced here: 66.1 us
  Pallas kernels  65.3 us (99%)
  between operations  0.8 us (1%)
    pallas_call x1, Pallas kernels, body(): pl.pallas_call(kernel, out_shape=made, in_specs=[any_] * 10, out_specs=(h...  63.6 us
    pallas_call x1, Pallas kernels, body(): pl.pallas_call(put_kernel, out_shape=(rows, rows, rows, rows, jax.ShapeDt...  1.72 us

profile of v2, /device:TPU:1, one launch (start us, length us, event | category | flops | bytes accessed | tf_op | source)
XLA Modules:
  0.0 66.1 jit_solution(16428590725597719560)
XLA Ops:
  0.6 63.6 %sketch_bwd.1 = (bf16[256,512]{1,0:T(8,128)(2,1)S(1)}, bf16[3,256,512]{2,1,0:T(8,128)(2,1)S(1)}, f32[8,64,1024]{2,1,0:T(8,128)S(1)}, f32[8,1024]{1,0:T(8,128)S(1)}) custom-call(bf16[256,512]{1,0:T(8,128)(2,1)} %x_hbm.1, bf16[2048,512]{1,0:T(8,128)(2,1)} %wq_hbm.1, bf16[2048,512]{1,0:T(8,128)(2,1)} %wk_hbm.1, bf16[2048,512]{1,0:T(8,128)(2,1)} %wv_hbm.1, ...), custom_call_target="tpu_custom_call" | custom-call | tf_op jit(solution)/shard_map/sketch_bwd/pallas_call | solution.py:745
  64.2 1.7 %put_out.1 = (bf16[256,512]{1,0:T(8,128)(2,1)}, bf16[256,512]{1,0:T(8,128)(2,1)}, bf16[256,512]{1,0:T(8,128)(2,1)}, bf16[256,512]{1,0:T(8,128)(2,1)}, f32[8,64,1024]{2,1,0:T(8,128)}, /*index=5*/f32[8,1024]{1,0:T(8,128)}) custom-call(bf16[256,512]{1,0:T(8,128)(2,1)S(1)} %get-tuple-element.16.oin, bf16[3,256,512]{2,1,0:T(8,128)(2,1)S(1)} %get-tuple-element.17.oqkv, ...), custom_call_target="tpu_custom_call" | custom-call | tf_op jit(solution)/shard_map/put_out/pallas_call | solution.py:760

commit v3 on v2

--- a/solution.py
+++ b/solution.py
@@ -38,7 +38,7 @@
     x_hbm, wq_hbm, wk_hbm, wv_hbm, g_hbm, ps_hbm, pn_hbm, da_hbm, de_hbm, dn_hbm,
     oin, oqkv, dps, dpn,
     xg, w, acc, qkv, xsend, ga, gt, psv, pnv, dev, dnv,
-    bd, bdh, bdl, bdt, lrt, skt, skb, stok, feat, vtm, vtok, dext, fold, stk, fsel,
+    bd, bdh, bdl, bdt, lrt, skt, skb, stok, st, feat, vtm, vtok, dext, fold, stk, fsel,
     yloc, gtr, scr, dmat, wmat, yv, tmp, zst, zpad, dfe, dst, dvt, sext, sextt, sextb,
     wire, inb, outb, res, totb, tot, dtok, dall, acc2, rsend, rrecv,
     loc, ag_s, ag_r, ex_s, ex_r, a_s, a_r, b_s, b_r, t_s, t_r, rs_s, rs_r,
@@ -94,7 +94,7 @@
 
     def slab(src, k, peer, i):
         ref = xg.at[2 * src + k]
-        return rc(ref, ref, ag_s, ag_r.at[i], head=peer)
+        return rc(ref, ref, ag_s.at[min(i, 2)], ag_r.at[i], head=peer)
 
     ag = [
         slab(x, 0, right, 0), slab(x, 1, left, 1), slab(x, 1, right, 2), slab(x, 0, left, 3),
@@ -102,7 +102,7 @@
     ]
     lx[0].wait()
     lx[1].wait()
-    for i in range(4):
+    for i in range(2):
         ag[i].start()
     cga = rc(da_hbm.at[:, oth_cols], ga.at[c], ex_s.at[0], ex_r.at[0], seq_2=oc)
     cga.start()
@@ -134,11 +134,6 @@
                 acc[t] += out
 
     project(x, True)
-    ag[0].wait_recv()
-    ag[4].start()
-    ag[1].wait_recv()
-    ag[5].start()
-
     def build(i, _):
         f = lax.broadcasted_iota(jnp.int32, (SK, 1024), 1)
         fi, fj = f // SK, lax.rem(f, SK)
@@ -162,6 +157,13 @@
     vtm[...] = jnp.zeros(vtm.shape, BF)
     sext[...] = jnp.zeros(sext.shape, F32)
 
+    for i in range(2):
+        ag[i].wait_send()
+        ag[2 + i].start()
+    ag[0].wait_recv()
+    ag[4].start()
+    ag[1].wait_recv()
+    ag[5].start()
     ag[2].wait_recv()
     project(left, False)
     ag[3].wait_recv()
@@ -202,8 +204,6 @@
         src = qkv[t, k]
         lr = nt(bdh[...], src) + nt(bdl[...], src)
         lrt[t, :, part] = lr
-        tok = nt(src, bdh[...]) + nt(src, bdl[...])
-        stok[t, part, :] = (tok[:, :128] * tok[:, 128:] * scale).astype(BF)
         st = lr[:128] * lr[128:] * scale
         skt[t, :, part] = st
         skb[t, :, part] = st.astype(BF)
@@ -221,7 +221,12 @@
 
         lax.fori_loop(0, 4, one, 0)
 
-    lane256 = lax.broadcasted_iota(jnp.int32, (CT, 256), 1)
+    def sketch_tokens(t):
+        for k in range(2):
+            tok = nt(qkv[t, k], bdh[...]) + nt(qkv[t, k], bdl[...])
+            stok[256 * k : 256 * k + 256, :] = (tok[:, :128] * tok[:, 128:] * scale).astype(BF)
+
+    lane256 = lax.broadcasted_iota(jnp.int32, (256, 256), 1)
 
     def pack_z(n, total):
         tmp[0:NF, :] = total
@@ -235,22 +240,19 @@
             py, pz = lax.rem(y + d // 4, 4), lax.rem(z + d % 4, 4)
             yield py * 4 + pz, {"seq_0": py, "seq_1": pz}
 
+    def rows_of(r):
+        return pl.ds(pl.multiple_of(r * ROWS, ROWS), ROWS)
+
     def scan_send(n, lo, hi):
         for r, where in others():
 
             @pl.when((r >= lo) & (r < hi))
             def _(r=r, where=where):
-                rc(
-                    wire.at[n, pl.ds(pl.multiple_of(r * ROWS, ROWS), ROWS)], inb.at[n, m],
-                    a_s.at[n], a_r.at[n], **where,
-                ).start()
+                rc(wire.at[n, rows_of(r)], inb.at[n, m], a_s.at[n], a_r.at[n], **where).start()
 
         @pl.when((m >= lo) & (m < hi))
         def _():
-            inb[n, m] = wire[n, pl.ds(pl.multiple_of(m * ROWS, ROWS), ROWS), :]
-
-    def mine(ref):
-        return ref.at[pl.ds(pl.multiple_of(m * ROWS, ROWS), ROWS)]
+            inb[n, m] = wire[n, rows_of(m), :]
 
     def scan_own(n, reverse):
         @pl.when(m < OWN)
@@ -265,12 +267,15 @@
             if reverse:
                 totb[...] = running.astype(BF)
             for r, where in others():
-                rc(outb.at[n, r], mine(res.at[n]), b_s.at[n], b_r.at[n], **where).start()
-            res[n, pl.ds(pl.multiple_of(m * ROWS, ROWS), ROWS), :] = outb[n, m]
-            if reverse:
-                tot[c, pl.ds(pl.multiple_of(m * ROWS, ROWS), ROWS), :] = totb[...]
-                for r, where in others():
-                    rc(totb, mine(tot.at[c]), t_s, t_r, **where).start()
+                rc(outb.at[n, r], res.at[n, rows_of(m)], b_s.at[n], b_r.at[n], **where).start()
+            res[n, rows_of(m), :] = outb[n, m]
+
+    def share_totals():
+        @pl.when(m < OWN)
+        def _():
+            for r, where in others():
+                rc(totb, tot.at[c, rows_of(m)], t_s, t_r, **where).start()
+            tot[c, rows_of(m), :] = totb[...]
 
     def from_owners(ref, sem):
         def all_of(count):
@@ -286,25 +291,20 @@
             all_of(OWN)
 
     def sends_done():
-        for n in range(2):
-            def all_of(count):
-                part = wire.at[n, pl.ds(0, count * ROWS)]
-                rc(part, part, a_s.at[n], t_r, seq_2=oc).wait_send()
-
-            @pl.when(m < OWN)
-            def _():
-                all_of(OWN - 1)
-                part = outb.at[n, 0 : CH - 1]
-                rc(part, part, b_s.at[n], t_r, seq_2=oc).wait_send()
-
-            @pl.when(m >= OWN)
-            def _():
-                all_of(OWN)
+        def all_of(part, sem):
+            rc(part, part, sem, t_r, seq_2=oc).wait_send()
 
         @pl.when(m < OWN)
         def _():
-            part = outb.at[0, 0 : CH - 1]
-            rc(part, part, t_s, t_r, seq_2=oc).wait_send()
+            for n in range(2):
+                all_of(wire.at[n, pl.ds(0, (OWN - 1) * ROWS)], a_s.at[n])
+                all_of(outb.at[n, 0 : CH - 1], b_s.at[n])
+            all_of(outb.at[0, 0 : CH - 1], t_s)
+
+        @pl.when(m >= OWN)
+        def _():
+            for n in range(2):
+                all_of(wire.at[n, pl.ds(0, OWN * ROWS)], a_s.at[n])
 
     def fold_in(state, norm):
         stk[0:256, :] = state
@@ -326,32 +326,40 @@
             sext[p, 0:NF, 128:256] = zc
             sextt[p] = jnp.transpose(sext[p])[0:144, :].astype(BF)
 
+    def state_half(k, last):
+        part = pl.ds(pl.multiple_of(256 * k, 256), 256)
+        for p in range(2):
+            vtok[p, part, 0:128] = qkv[2, k, :, 128 * p : 128 * p + 128]
+            vtok[p, part, 128:256] = jnp.ones((256, 128), BF)
+        ztot = None
+        for p in range(2):
+            out = st[p] if last else None
+            for hh in range(2):
+                h = 2 * p + hh
+                keep = (lane256 // 64 == hh) | (lane256 == 128 + h)
+                vm = jnp.where(keep, vtok[p, part, :].astype(F32), 0.0).astype(BF)
+                term = nn(feat[1, h, 0:NF, part], vm)
+                out = term if out is None else out + term
+            if not last:
+                st[p] = out
+                continue
+            wire[0, NF * p : NF * p + NF, :] = out[:, 0:128].astype(BF)
+            ztot = out[:, 128:256] if ztot is None else ztot + out[:, 128:256]
+            if p == 0:
+                scan_send(0, 0, SPLIT)
+        if last:
+            pack_z(0, ztot)
+            scan_send(0, SPLIT, OWN)
+
     sketch(1, c)
+    state_half(c, False)
     cqkv[1].wait_recv()
     sketch(1, oc)
     cqkv[2].wait_recv()
-    for p in range(2):
-        for k in range(2):
-            vtok[p, 256 * k : 256 * k + 256, 0:128] = qkv[2, k, :, 128 * p : 128 * p + 128]
-        vtok[p, :, 128:256] = jnp.ones((CT, 128), BF)
-    ztot = None
-    for p in range(2):
-        out = None
-        for hh in range(2):
-            h = 2 * p + hh
-            keep = (lane256 // 64 == hh) | (lane256 == 128 + h)
-            vm = jnp.where(keep, vtok[p].astype(F32), 0.0).astype(BF)
-            part = nn(feat[1, h, 0:NF, :], vm)
-            out = part if out is None else out + part
-        wire[0, NF * p : NF * p + NF, :] = out[:, 0:128].astype(BF)
-        ztot = out[:, 128:256] if ztot is None else ztot + out[:, 128:256]
-        if p == 0:
-            scan_send(0, 0, SPLIT)
-    pack_z(0, ztot)
-    scan_send(0, SPLIT, OWN)
-
+    state_half(oc, True)
 
     last_projection(0)
+    sketch_tokens(1)
     lp.wait()
     ln.wait()
     fold_in(psv[...].reshape(256, 1024).astype(BF), pnv)
@@ -380,7 +388,7 @@
 
     def scores(h, _):
         for jb in range(2):
-            keys = jnp.where(lane_k == h, stok[1, 256 * jb : 256 * jb + 256, :].astype(F32), 0.0)
+            keys = jnp.where(lane_k == h, stok[256 * jb : 256 * jb + 256, :].astype(F32), 0.0)
             keys = keys.astype(BF)
             for ib in range(jb, 2):
                 d = nn(keys, skb[0, :, 256 * ib : 256 * ib + 256])
@@ -497,9 +505,9 @@
     lax.fori_loop(0, 4, local_grads, 0)
 
     copy_q = []
-    for u in range(2):
-
-        def grad_q(p, _, u=u):
+
+    def queries_half(u):
+        def grad_q(p, _):
             for hh in range(2):
                 h = 2 * p + hh
                 dfe[hh] = nn(sext[p, 0:NF, :].astype(BF), lanes(dext.at[h], (slice(0, 256),), u))
@@ -509,7 +517,10 @@
         lax.fori_loop(0, 2, grad_q, 0)
         keep(0, u, through_sketch(0, u))
         copy_q.append(hand_q(u))
+
+    queries_half(0)
     scan_own(1, True)
+    queries_half(1)
 
     le.wait()
     lm.wait()
@@ -517,22 +528,18 @@
     for u in range(2):
         copy_q[u].wait_recv()
 
-    def pull(t, b, rows):
-        out = None
-        for k in range(2):
-            part = nt(
-                dall[t, k, rows], w[t, pl.ds(pl.multiple_of(b * 512, 512), 512), 256 * k : 256 * k + 256]
-            )
-            out = part if out is None else out + part
-        return out
+    def pull(t, b, rows, k):
+        cols = pl.ds(pl.multiple_of(256 * k, 256), 256)
+        return nt(dall[t, k, rows], w[t, pl.ds(pl.multiple_of(b * 512, 512), 512), cols])
 
     def pull_q(b, _):
-        acc2[b] = pull(0, b, slice(0, 256))
+        acc2[b] = pull(0, b, slice(0, 256), 0) + pull(0, b, slice(0, 256), 1)
         return 0
 
     lax.fori_loop(0, 4, pull_q, 0)
 
     from_owners(res.at[1], b_r.at[1])
+    share_totals()
     unpack(1)
 
     def grads(u):
@@ -566,13 +573,18 @@
         for u in range(2)
     ]
 
-    def block(b, u):
+    def block(b, u, ahead=False):
         rows = slice(128 * u, 128 * u + 128)
-        return acc2[b, rows, :] + pull(1, b, rows) + pull(2, b, rows)
+        out = acc2[b, rows, :] + pull(1, b, rows, oc) + pull(2, b, rows, oc)
+        return out if ahead else out + pull(1, b, rows, c) + pull(2, b, rows, c)
+
+    def own_part(b, u):
+        rows = slice(128 * u, 128 * u + 128)
+        acc2[b, rows, :] += pull(1, b, rows, c) + pull(2, b, rows, c)
 
     def outgoing(u):
         rows = slice(128 * u, 128 * u + 128)
-        out = block(far, u)
+        out = block(far, u, u == 0)
         rsend[u, 0] = out[:, 0:256].astype(BF)
         rs[u][0].start()
         rsend[u, 1] = out[:, 256:512].astype(BF)
@@ -608,6 +620,7 @@
             acc2[x, rows, 256:512] + rrecv[u, 2].astype(F32) + rrecv[u, 5].astype(F32)
         ).astype(BF)
 
+    own_part(far, 0)
     copy_kv[0].wait_recv()
     outgoing(0)
     copy_kv[1].wait_recv()
@@ -646,8 +659,8 @@
     arrived(0)
     arrived(1)
 
-    sends = xg.at[0:6]
-    rc(sends, sends, ag_s, t_r, seq_2=oc).wait_send()
+    sends = xg.at[0:4]
+    rc(sends, sends, ag_s.at[2], t_r, seq_2=oc).wait_send()
     for one in list(cqkv.values()) + [cga, copy_t] + copy_q + copy_kv:
         one.wait_send()
     sends = rsend.at[:]
@@ -694,7 +707,8 @@
         v((2, 256, CT), F32),
         v((2, 128, CT), F32),
         v((2, 128, CT), BF),
-        v((2, CT, 128), BF),
+        v((CT, 128), BF),
+        v((2, NF, 256), F32),
         v((2, 4, NP, CT), BF),
         v((4, 256, CT), BF),
         v((2, CT, 256), BF),
@@ -731,7 +745,7 @@
     ]
     sem = pltpu.SemaphoreType.DMA
     scratch += [
-        sem((11,)), sem, sem((6,)), sem((9,)), sem((9,)), sem((2,)), sem((2,)),
+        sem((11,)), sem((3,)), sem((6,)), sem((9,)), sem((9,)), sem((2,)), sem((2,)),
         sem((2,)), sem((2,)), sem, sem, sem, sem((2, 6)),
     ]
     swap = (0, 2, 1)

time: 66.2 us -> 64.2 us (0.970)
  Pallas kernels: 65.3 us -> 63.3 us
    pallas_call x1, Pallas kernels: 63.6 us -> 61.6 us  [body(): pl.pallas_call(kernel, out_shape=made, in_specs=[any_] * 10, out_specs=(h...]
where the time goes in v3:
time: 64.2 us; the launch traced here: 64.1 us
  Pallas kernels  63.3 us (99%)
  between operations  0.8 us (1%)
    pallas_call x1, Pallas kernels, body(): pl.pallas_call(kernel, out_shape=made, in_specs=[any_] * 10, out_specs=(h...  61.6 us
    pallas_call x1, Pallas kernels, body(): pl.pallas_call(put_kernel, out_shape=(rows, rows, rows, rows, jax.ShapeDt...  1.72 us

profile of v3, /device:TPU:1, one launch (start us, length us, event | category | flops | bytes accessed | tf_op | source)
XLA Modules:
  0.0 64.1 jit_solution(15205856373210290293)
XLA Ops:
  0.6 61.6 %sketch_bwd.1 = (bf16[256,512]{1,0:T(8,128)(2,1)S(1)}, bf16[3,256,512]{2,1,0:T(8,128)(2,1)S(1)}, f32[8,64,1024]{2,1,0:T(8,128)S(1)}, f32[8,1024]{1,0:T(8,128)S(1)}) custom-call(bf16[256,512]{1,0:T(8,128)(2,1)} %x_hbm.1, bf16[2048,512]{1,0:T(8,128)(2,1)} %wq_hbm.1, bf16[2048,512]{1,0:T(8,128)(2,1)} %wk_hbm.1, bf16[2048,512]{1,0:T(8,128)(2,1)} %wv_hbm.1, ...), custom_call_target="tpu_custom_call" | custom-call | tf_op jit(solution)/shard_map/sketch_bwd/pallas_call | solution.py:759
  62.2 1.7 %put_out.1 = (bf16[256,512]{1,0:T(8,128)(2,1)}, bf16[256,512]{1,0:T(8,128)(2,1)}, bf16[256,512]{1,0:T(8,128)(2,1)}, bf16[256,512]{1,0:T(8,128)(2,1)}, f32[8,64,1024]{2,1,0:T(8,128)}, /*index=5*/f32[8,1024]{1,0:T(8,128)}) custom-call(bf16[256,512]{1,0:T(8,128)(2,1)S(1)} %get-tuple-element.16.oin, bf16[3,256,512]{2,1,0:T(8,128)(2,1)S(1)} %get-tuple-element.17.oqkv, ...), custom_call_target="tpu_custom_call" | custom-call | tf_op jit(solution)/shard_map/put_out/pallas_call | solution.py:774

commit v4 on v3

--- a/solution.py
+++ b/solution.py
@@ -204,22 +204,19 @@
         src = qkv[t, k]
         lr = nt(bdh[...], src) + nt(bdl[...], src)
         lrt[t, :, part] = lr
-        st = lr[:128] * lr[128:] * scale
-        skt[t, :, part] = st
-        skb[t, :, part] = st.astype(BF)
-
-        def one(h, _):
+        st_ = lr[:128] * lr[128:] * scale
+        skt[t, :, part] = st_
+        skb[t, :, part] = st_.astype(BF)
+
+        for h in range(4):
             for q in range(2):
                 cols = pl.ds(pl.multiple_of(256 * k + 128 * q, 128), 128)
-                s = skt[t, pl.ds(pl.multiple_of(h * SK, SK), SK), cols]
+                s = st_[SK * h : SK * h + SK, 128 * q : 128 * q + 128]
                 for b in range(8):
                     turned = ones(s, b)
                     for a in range(3 if b == 0 else 2):
                         i = 8 * a + b
                         feat[t, h, SK * i : SK * i + SK, cols] = (s * eights(turned, a)).astype(BF)
-            return 0
-
-        lax.fori_loop(0, 4, one, 0)
 
     def sketch_tokens(t):
         for k in range(2):
@@ -306,11 +303,11 @@
             for n in range(2):
                 all_of(wire.at[n, pl.ds(0, OWN * ROWS)], a_s.at[n])
 
-    def fold_in(state, norm):
+    def fold_in(n, state, norm):
         stk[0:256, :] = state
         pick = jnp.where(c == 0, norm[0:4, :], norm[4:8, :])
         stk[256:272, :] = jnp.concatenate([pick, jnp.zeros((12, 1024), F32)], axis=0).astype(BF)
-        fold[...] = nt(fsel[...], stk[...])
+        fold[n] = nt(fsel[...], stk[...])
 
     row_w = lax.broadcasted_iota(jnp.int32, (NF, 128), 0)
     weight = jnp.where((row_w < SK) | (row_w >= 16 * SK), 1.0, 2.0)
@@ -319,12 +316,15 @@
         zst[...] = res[n, ZROW:WIRE, :].astype(F32)
         for j in range(5):
             zpad[0:4, 128 * j : 128 * j + 128] = zst[4 * j : 4 * j + 4, :]
-        zc = jnp.transpose(zpad[...])[0:NF, :] * weight + fold[0:NF, 256:384]
+        zc = jnp.transpose(zpad[...])[0:NF, :] * weight + fold[n, 0:NF, 256:384]
         for p in range(2):
             part = res[n, NF * p : NF * p + NF, :].astype(F32)
-            sext[p, 0:NF, 0:128] = part * weight + fold[0:NF, 128 * p : 128 * p + 128]
+            sext[p, 0:NF, 0:128] = part * weight + fold[n, 0:NF, 128 * p : 128 * p + 128]
             sext[p, 0:NF, 128:256] = zc
-            sextt[p] = jnp.transpose(sext[p])[0:144, :].astype(BF)
+            turned = jnp.transpose(sext[p]).astype(BF)
+            for hh in range(2):
+                sextt[2 * p + hh, 0:64, :] = turned[64 * hh : 64 * hh + 64, :]
+                sextt[2 * p + hh, 64:80, :] = turned[128:144, :]
 
     def state_half(k, last):
         part = pl.ds(pl.multiple_of(256 * k, 256), 256)
@@ -362,7 +362,7 @@
     sketch_tokens(1)
     lp.wait()
     ln.wait()
-    fold_in(psv[...].reshape(256, 1024).astype(BF), pnv)
+    fold_in(0, psv[...].reshape(256, 1024).astype(BF), pnv)
     sketch(0, c)
     cqkv[0].wait_recv()
     sketch(0, oc)
@@ -386,7 +386,8 @@
     )
     lane_k = lax.broadcasted_iota(jnp.int32, (256, 128), 1) // SK
 
-    def scores(h, _):
+    def scores(h, hh):
+        d_rows = slice(64 * hh, 64 * hh + 64)
         for jb in range(2):
             keys = jnp.where(lane_k == h, stok[256 * jb : 256 * jb + 256, :].astype(F32), 0.0)
             keys = keys.astype(BF)
@@ -397,28 +398,37 @@
                 at = (h, slice(256 * jb, 256 * jb + 256), slice(256 * ib, 256 * ib + 256))
                 scr[at] = (d * d).astype(BF)
                 dmat[at] = (d + d).astype(BF)
-        yloc[h, :, 0:256] = nn(vtm[h, 0:144, 0:256], scr[h, 0:256, 0:256])
-        yloc[h, :, 256:512] = nn(vtm[h, 0:144, :], scr[h, :, 256:512])
-        return 0
-
-    lax.fori_loop(0, 4, scores, 0)
+        values = jnp.concatenate([vtm[h, d_rows, :], vtm[h, 128:144, :]], axis=0)
+        yloc[h, :, 0:256] = nn(values[:, 0:256], scr[h, 0:256, 0:256])
+        yloc[h, :, 256:512] = nn(values, scr[h, :, 256:512])
+
+    def by_pairs(make):
+        def one(p, _):
+            for hh in range(2):
+                make(2 * p + hh, hh)
+            return 0
+
+        lax.fori_loop(0, 2, one, 0)
+
+    by_pairs(scores)
+    le.wait()
+    lm.wait()
+    fold_in(1, dev[pl.ds(4 * c, 4)].reshape(256, 1024).astype(BF), dnv)
 
     from_owners(res.at[0], b_r.at[0])
     unpack(0)
+    for h in range(4):
+        yv[h] = nn(sextt[h], feat[0, h]) + yloc[h]
+    for h in range(4):
+        inv = 1.0 / (1.0 + yv[h, 64 + h : 65 + h, :])
+        g = gtr[64 * h : 64 * h + 64, :]
+        dden = -jnp.sum(g * yv[h, 0:64, :], axis=0, keepdims=True) * inv * inv
+        dext[h, 64 * (h % 2) : 64 * (h % 2) + 64, :] = (g * inv).astype(BF)
+        dext[h, 128:144, :] = jnp.where(row16 == h, dden, 0.0).astype(BF)
     ztot = None
     for p in range(2):
-        out = None
-        for hh in range(2):
-            h = 2 * p + hh
-            yv[h] = nn(sextt[p], feat[0, h]) + yloc[h]
-            num = yv[h, 64 * hh : 64 * hh + 64, :]
-            inv = 1.0 / (1.0 + yv[h, 128 + h : 129 + h, :])
-            g = gtr[64 * h : 64 * h + 64, :]
-            dden = -jnp.sum(g * num, axis=0, keepdims=True) * inv * inv
-            dext[h, 64 * hh : 64 * hh + 64, :] = (g * inv).astype(BF)
-            dext[h, 128:144, :] = jnp.where(row16 == h, dden, 0.0).astype(BF)
-            part = nt(feat[0, h, 0:NF, :], dext[h])
-            out = part if out is None else out + part
+        out = nt(feat[0, 2 * p, 0:NF, :], dext[2 * p])
+        out = out + nt(feat[0, 2 * p + 1, 0:NF, :], dext[2 * p + 1])
         wire[1, NF * p : NF * p + NF, :] = out[:, 0:128].astype(BF)
         ztot = out[:, 128:256] if ztot is None else ztot + out[:, 128:256]
         if p == 0:
@@ -453,7 +463,7 @@
                 here = here + (back if b == 0 else pltpu.roll(back, b, 0))
             dst[t, rows, cols] = here
 
-    def local_grads(h, _):
+    def local_grads(h, hh):
         p = h // 2
         for jb in range(2):
             for ib in range(jb, 2):
@@ -461,7 +471,7 @@
                 ds = nn(vtok[p, 256 * jb : 256 * jb + 256, :], dext[h, :, 256 * ib : 256 * ib + 256])
                 wmat[at] = (dmat[at].astype(F32) * ds).astype(BF)
         sk_rows = pl.ds(pl.multiple_of(h * SK, SK), SK)
-        d_rows = pl.ds(pl.multiple_of(64 * lax.rem(h, 2), 64), 64)
+        d_rows = slice(64 * hh, 64 * hh + 64)
         v_rows = pl.ds(pl.multiple_of(64 * h, 64), 64)
         dst[0, sk_rows, 0:256] = nn(skb[1, sk_rows, 0:256], wmat[h, 0:256, 0:256])
         dst[0, sk_rows, 256:512] = nn(skb[1, sk_rows, :], wmat[h, :, 256:512])
@@ -469,7 +479,6 @@
         dst[1, sk_rows, 256:512] = nt(skb[0, sk_rows, 256:512], wmat[h, 256:512, 256:512])
         dvt[v_rows, 0:256] = nt(dext[h, d_rows, :], scr[h, 0:256, :])
         dvt[v_rows, 256:512] = nt(dext[h, d_rows, 256:512], scr[h, 256:512, 256:512])
-        return 0
 
     def through_sketch(t, u):
         at = (slice(0, 128),)
@@ -502,7 +511,7 @@
         copy.start()
         return copy
 
-    lax.fori_loop(0, 4, local_grads, 0)
+    by_pairs(local_grads)
 
     copy_q = []
 
@@ -522,9 +531,6 @@
     scan_own(1, True)
     queries_half(1)
 
-    le.wait()
-    lm.wait()
-    fold_in(dev[pl.ds(4 * c, 4)].reshape(256, 1024).astype(BF), dnv)
     for u in range(2):
         copy_q[u].wait_recv()
 
@@ -543,17 +549,20 @@
     unpack(1)
 
     def grads(u):
+        def key_state(h):
+            dfe[h] = nn(sextb[h // 2], lanes(vtm.at[h], (slice(0, 256),), u))
+
+        key_state(0)
         for h in range(4):
+            if h < 3:
+                key_state(h + 1)
             v_rows = slice(64 * h, 64 * h + 64)
-            d_rows = slice(64 * (h % 2), 64 * (h % 2) + 64)
-            out = nn(sextt[h // 2, d_rows, :], lanes(feat.at[1, h], (slice(0, NP),), u))
+            out = nn(sextt[h, 0:64, :], lanes(feat.at[1, h], (slice(0, NP),), u))
             for q in range(2):
                 cols = slice(256 * q + 128 * u, 256 * q + 128 * u + 128)
                 dvt[v_rows, cols] += out[:, 128 * q : 128 * q + 128]
+            feature_grad(1, h, u, h)
         keep(2, u, lanes(dvt, (slice(0, 256),), u))
-        for h in range(4):
-            dfe[h] = nn(sextb[h // 2], lanes(vtm.at[h], (slice(0, 256),), u))
-            feature_grad(1, h, u, h)
         keep(1, u, through_sketch(1, u))
         return hand_kv(u)
 
@@ -713,15 +722,15 @@
         v((4, 256, CT), BF),
         v((2, CT, 256), BF),
         v((4, 256, CT), BF),
-        v((NP, 384), F32),
+        v((2, NP, 384), F32),
         v((384, 1024), BF),
         v((NP, 1024), BF),
-        v((4, 144, CT), F32),
+        v((4, 80, CT), F32),
         v((256, CT), F32),
         v((4, CT, CT), BF),
         v((4, CT, CT), BF),
         v((4, CT, CT), BF),
-        v((4, 144, CT), F32),
+        v((4, 80, CT), F32),
         v((NP, 128), F32),
         v((SK, 128), F32),
         v((128, NP), F32),
@@ -729,7 +738,7 @@
         v((2, 128, CT), F32),
         v((256, CT), F32),
         v((2, NP, 256), F32),
-        v((2, 144, NP), BF),
+        v((4, 80, NP), BF),
         v((2, NF, 256), BF),
         v((2, WIRE, 128), BF),
         v((2, CH, ROWS, 128), BF),

time: 64.2 us -> 63.6 us (level)
  no operation moved by 1% of the time
where the time goes in v4:
time: 63.6 us; the launch traced here: 63.5 us
  Pallas kernels  62.7 us (99%)
  between operations  0.8 us (1%)
    pallas_call x1, Pallas kernels, body(): pl.pallas_call(kernel, out_shape=made, in_specs=[any_] * 10, out_specs=(h...  61 us
    pallas_call x1, Pallas kernels, body(): pl.pallas_call(put_kernel, out_shape=(rows, rows, rows, rows, jax.ShapeDt...  1.72 us

profile of v4, /device:TPU:1, one launch (start us, length us, event | category | flops | bytes accessed | tf_op | source)
XLA Modules:
  0.0 63.5 jit_solution(9069125768005832830)
XLA Ops:
  0.6 61.0 %sketch_bwd.1 = (bf16[256,512]{1,0:T(8,128)(2,1)S(1)}, bf16[3,256,512]{2,1,0:T(8,128)(2,1)S(1)}, f32[8,64,1024]{2,1,0:T(8,128)S(1)}, f32[8,1024]{1,0:T(8,128)S(1)}) custom-call(bf16[256,512]{1,0:T(8,128)(2,1)} %x_hbm.1, bf16[2048,512]{1,0:T(8,128)(2,1)} %wq_hbm.1, bf16[2048,512]{1,0:T(8,128)(2,1)} %wk_hbm.1, bf16[2048,512]{1,0:T(8,128)(2,1)} %wv_hbm.1, ...), custom_call_target="tpu_custom_call" | custom-call | tf_op jit(solution)/shard_map/sketch_bwd/pallas_call | solution.py:768
  61.6 1.7 %put_out.1 = (bf16[256,512]{1,0:T(8,128)(2,1)}, bf16[256,512]{1,0:T(8,128)(2,1)}, bf16[256,512]{1,0:T(8,128)(2,1)}, bf16[256,512]{1,0:T(8,128)(2,1)}, f32[8,64,1024]{2,1,0:T(8,128)}, /*index=5*/f32[8,1024]{1,0:T(8,128)}) custom-call(bf16[256,512]{1,0:T(8,128)(2,1)S(1)} %get-tuple-element.16.oin, bf16[3,256,512]{2,1,0:T(8,128)(2,1)S(1)} %get-tuple-element.17.oqkv, ...), custom_call_target="tpu_custom_call" | custom-call | tf_op jit(solution)/shard_map/put_out/pallas_call | solution.py:783

commit v5 on v4

--- a/solution.py
+++ b/solution.py
@@ -23,7 +23,6 @@
 WIRE = OWN * ROWS
 FAR_FIRST = (10, 9, 11, 6, 14, 2, 8, 5, 7, 13, 15, 1, 3, 4, 12)
 ZROW = 2 * NF
-SPLIT = NF // ROWS
 
 
 def nn(a, b):
@@ -184,9 +183,9 @@
             )
             if target is None:
                 xsend[t] = out.astype(BF)
-                cqkv[t].start()
             else:
                 qkv[t, target] = out.astype(BF)
+        cqkv[t].start()
 
     last_projection(1)
     last_projection(2)
@@ -345,11 +344,9 @@
                 continue
             wire[0, NF * p : NF * p + NF, :] = out[:, 0:128].astype(BF)
             ztot = out[:, 128:256] if ztot is None else ztot + out[:, 128:256]
-            if p == 0:
-                scan_send(0, 0, SPLIT)
         if last:
             pack_z(0, ztot)
-            scan_send(0, SPLIT, OWN)
+            scan_send(0, 0, OWN)
 
     sketch(1, c)
     state_half(c, False)
@@ -431,10 +428,8 @@
         out = out + nt(feat[0, 2 * p + 1, 0:NF, :], dext[2 * p + 1])
         wire[1, NF * p : NF * p + NF, :] = out[:, 0:128].astype(BF)
         ztot = out[:, 128:256] if ztot is None else ztot + out[:, 128:256]
-        if p == 0:
-            scan_send(1, 0, SPLIT)
     pack_z(1, ztot)
-    scan_send(1, SPLIT, OWN)
+    scan_send(1, 0, OWN)
 
     def lanes(ref, at, u):
         return jnp.concatenate(
@@ -598,14 +593,14 @@
         rs[u][0].start()
         rsend[u, 1] = out[:, 256:512].astype(BF)
         rs[u][1].start()
-        out = block(right, u)
-        rsend[u, 2] = out[:, 256:512].astype(BF)
+        out_r = block(right, u)
+        out_l = block(left, u)
+        rsend[u, 2] = out_r[:, 256:512].astype(BF)
+        rsend[u, 3] = out_l[:, 0:256].astype(BF)
+        acc2[right, rows, 0:256] = out_r[:, 0:256]
+        acc2[left, rows, 256:512] = out_l[:, 256:512]
         rs[u][2].start()
-        acc2[right, rows, 0:256] = out[:, 0:256]
-        out = block(left, u)
-        rsend[u, 3] = out[:, 0:256].astype(BF)
         rs[u][3].start()
-        acc2[left, rows, 256:512] = out[:, 256:512]
 
     def merge(u):
         rows = slice(128 * u, 128 * u + 128)

time: 63.6 us -> 62.9 us (0.989)
  Pallas kernels: 62.7 us -> 61.9 us
    pallas_call x1, Pallas kernels: 61 us -> 60.2 us  [body(): pl.pallas_call(kernel, out_shape=made, in_specs=[any_] * 10, out_specs=(h...]
where the time goes in v5:
time: 62.9 us; the launch traced here: 62.7 us
  Pallas kernels  61.9 us (98%)
  between operations  0.8 us (1%)
    pallas_call x1, Pallas kernels, body(): pl.pallas_call(kernel, out_shape=made, in_specs=[any_] * 10, out_specs=(h...  60.2 us
    pallas_call x1, Pallas kernels, body(): pl.pallas_call(put_kernel, out_shape=(rows, rows, rows, rows, jax.ShapeDt...  1.72 us

profile of v5, /device:TPU:1, one launch (start us, length us, event | category | flops | bytes accessed | tf_op | source)
XLA Modules:
  0.0 62.7 jit_solution(12699994228285833763)
XLA Ops:
  0.6 60.2 %sketch_bwd.1 = (bf16[256,512]{1,0:T(8,128)(2,1)S(1)}, bf16[3,256,512]{2,1,0:T(8,128)(2,1)S(1)}, f32[8,64,1024]{2,1,0:T(8,128)S(1)}, f32[8,1024]{1,0:T(8,128)S(1)}) custom-call(bf16[256,512]{1,0:T(8,128)(2,1)} %x_hbm.1, bf16[2048,512]{1,0:T(8,128)(2,1)} %wq_hbm.1, bf16[2048,512]{1,0:T(8,128)(2,1)} %wk_hbm.1, bf16[2048,512]{1,0:T(8,128)(2,1)} %wv_hbm.1, ...), custom_call_target="tpu_custom_call" | custom-call | tf_op jit(solution)/shard_map/sketch_bwd/pallas_call | solution.py:763
  60.9 1.7 %put_out.1 = (bf16[256,512]{1,0:T(8,128)(2,1)}, bf16[256,512]{1,0:T(8,128)(2,1)}, bf16[256,512]{1,0:T(8,128)(2,1)}, bf16[256,512]{1,0:T(8,128)(2,1)}, f32[8,64,1024]{2,1,0:T(8,128)}, /*index=5*/f32[8,1024]{1,0:T(8,128)}) custom-call(bf16[256,512]{1,0:T(8,128)(2,1)S(1)} %get-tuple-element.16.oin, bf16[3,256,512]{2,1,0:T(8,128)(2,1)S(1)} %get-tuple-element.17.oqkv, ...), custom_call_target="tpu_custom_call" | custom-call | tf_op jit(solution)/shard_map/put_out/pallas_call | solution.py:778

commit v6 on v4

--- a/solution.py
+++ b/solution.py
@@ -23,7 +23,6 @@
 WIRE = OWN * ROWS
 FAR_FIRST = (10, 9, 11, 6, 14, 2, 8, 5, 7, 13, 15, 1, 3, 4, 12)
 ZROW = 2 * NF
-SPLIT = NF // ROWS
 
 
 def nn(a, b):
@@ -184,9 +183,9 @@
             )
             if target is None:
                 xsend[t] = out.astype(BF)
-                cqkv[t].start()
             else:
                 qkv[t, target] = out.astype(BF)
+        cqkv[t].start()
 
     last_projection(1)
     last_projection(2)
@@ -345,11 +344,9 @@
                 continue
             wire[0, NF * p : NF * p + NF, :] = out[:, 0:128].astype(BF)
             ztot = out[:, 128:256] if ztot is None else ztot + out[:, 128:256]
-            if p == 0:
-                scan_send(0, 0, SPLIT)
         if last:
             pack_z(0, ztot)
-            scan_send(0, SPLIT, OWN)
+            scan_send(0, 0, OWN)
 
     sketch(1, c)
     state_half(c, False)
@@ -431,10 +428,8 @@
         out = out + nt(feat[0, 2 * p + 1, 0:NF, :], dext[2 * p + 1])
         wire[1, NF * p : NF * p + NF, :] = out[:, 0:128].astype(BF)
         ztot = out[:, 128:256] if ztot is None else ztot + out[:, 128:256]
-        if p == 0:
-            scan_send(1, 0, SPLIT)
     pack_z(1, ztot)
-    scan_send(1, SPLIT, OWN)
+    scan_send(1, 0, OWN)
 
     def lanes(ref, at, u):
         return jnp.concatenate(

time: 63.6 us -> 62.8 us (0.987)
  Pallas kernels: 62.7 us -> 61.8 us
    pallas_call x1, Pallas kernels: 61 us -> 60.1 us  [body(): pl.pallas_call(kernel, out_shape=made, in_specs=[any_] * 10, out_specs=(h...]
where the time goes in v6:
time: 62.8 us; the launch traced here: 62.6 us
  Pallas kernels  61.8 us (98%)
  between operations  0.8 us (1%)
    pallas_call x1, Pallas kernels, body(): pl.pallas_call(kernel, out_shape=made, in_specs=[any_] * 10, out_specs=(h...  60.1 us
    pallas_call x1, Pallas kernels, body(): pl.pallas_call(put_kernel, out_shape=(rows, rows, rows, rows, jax.ShapeDt...  1.72 us

profile of v6, /device:TPU:1, one launch (start us, length us, event | category | flops | bytes accessed | tf_op | source)
XLA Modules:
  0.0 62.6 jit_solution(13296633736611018692)
XLA Ops:
  0.6 60.1 %sketch_bwd.1 = (bf16[256,512]{1,0:T(8,128)(2,1)S(1)}, bf16[3,256,512]{2,1,0:T(8,128)(2,1)S(1)}, f32[8,64,1024]{2,1,0:T(8,128)S(1)}, f32[8,1024]{1,0:T(8,128)S(1)}) custom-call(bf16[256,512]{1,0:T(8,128)(2,1)} %x_hbm.1, bf16[2048,512]{1,0:T(8,128)(2,1)} %wq_hbm.1, bf16[2048,512]{1,0:T(8,128)(2,1)} %wk_hbm.1, bf16[2048,512]{1,0:T(8,128)(2,1)} %wv_hbm.1, ...), custom_call_target="tpu_custom_call" | custom-call | tf_op jit(solution)/shard_map/sketch_bwd/pallas_call | solution.py:763
  60.8 1.7 %put_out.1 = (bf16[256,512]{1,0:T(8,128)(2,1)}, bf16[256,512]{1,0:T(8,128)(2,1)}, bf16[256,512]{1,0:T(8,128)(2,1)}, bf16[256,512]{1,0:T(8,128)(2,1)}, f32[8,64,1024]{2,1,0:T(8,128)}, /*index=5*/f32[8,1024]{1,0:T(8,128)}) custom-call(bf16[256,512]{1,0:T(8,128)(2,1)S(1)} %get-tuple-element.16.oin, bf16[3,256,512]{2,1,0:T(8,128)(2,1)S(1)} %get-tuple-element.17.oqkv, ...), custom_call_target="tpu_custom_call" | custom-call | tf_op jit(solution)/shard_map/put_out/pallas_call | solution.py:778
